TPU v7x, 32 devices: a 4x2x2 block of a 4x4x8 slice. The times are simulated.
32 devices in a mesh: dp: 4 (over y, z), tp: 8 (over x, core).
Axes of the slice: x: 4, y: 2, z: 2, core: 2. Of those that a mesh axis runs over, the one named last changes fastest.
The devices are a block of a 4x4x8 slice.
Arguments:
- hidden: bfloat16 [4, 2048, 2048], P('dp', 'tp'), parts along dimension 0
- positions: int32 [4, 2048], P('dp'), parts along dimension 0
- norm_w: float32 [2048], replicated
- w_query: bfloat16 [2048, 2048], P(None, 'tp')
- w_key: bfloat16 [2048, 256], replicated
- w_value: bfloat16 [2048, 256], replicated
- w_out: bfloat16 [2048, 2048], P('tp')
- grad_out: bfloat16 [4, 2048, 2048], P('dp', 'tp'), parts along dimension 0
Outputs:
- output 1: bfloat16 [4, 2048, 2048], P('dp', 'tp'), parts along dimension 0
- output 2: bfloat16 [4, 2048, 2048], P('dp', 'tp'), parts along dimension 0
- output 3: float32 [8192, 2048], P('dp', 'tp'), parts along dimension 0
- output 4: float32 [8192, 2048], P(('dp', 'tp')), parts along dimension 0
- output 5: float32 [8192, 256], P('dp'), parts along dimension 0
- output 6: float32 [8192, 256], P('dp'), parts along dimension 0
- output 7: float32 [8192], P('dp'), parts along dimension 0
There are 4 independent parts. A program takes and returns all parts, laid end to end along the dimension named above; an argument that names none is the same for every part.
All inputs are finite; a program needn't handle non-finite values.
Results may differ from a plain program's by a relative error of at most 0.02.
Values are sent between devices in bfloat16 or wider.
A program may use at most 768 MiB of HBM per device.

v0:
```python
import jax
import jax.numpy as jnp
from jax import lax
from jax.sharding import PartitionSpec as P


def rope_tables(positions, head_dim):
    half = head_dim // 2
    inv_freq = 10000.0 ** (-2.0 * jnp.arange(half, dtype=jnp.float32) / head_dim)
    angle = positions.astype(jnp.float32)[..., None] * inv_freq
    return jnp.cos(angle), jnp.sin(angle)


def apply_rope(vector, cos_t, sin_t):
    half = vector.shape[-1] // 2
    first = vector[..., :half]
    second = vector[..., half:]
    return jnp.concatenate([first * cos_t - second * sin_t, second * cos_t + first * sin_t], axis=-1)


def local_block(hidden, positions, norm_w, w_query, w_key, w_value, w_out, grad_out):
    batch = hidden.shape[0]
    seq_len = positions.shape[1]
    head_dim = w_key.shape[1]
    heads_dev = w_query.shape[1] // head_dim
    scale = head_dim ** -0.5
    hidden_f = hidden.astype(jnp.float32)
    inv_rms = lax.rsqrt(jnp.mean(hidden_f * hidden_f, axis=-1, keepdims=True) + 1e-6)
    normed = hidden_f * inv_rms
    gain = 1.0 + norm_w
    act_local = (normed * gain).astype(jnp.bfloat16)
    act_full = lax.all_gather(act_local, 'tp', axis=1, tiled=True)
    query = jnp.einsum('bsd,de->bse', act_full, w_query, preferred_element_type=jnp.float32).astype(jnp.bfloat16).reshape(batch, seq_len, heads_dev, head_dim)
    key_proj = jnp.einsum('bsd,de->bse', act_full, w_key, preferred_element_type=jnp.float32).astype(jnp.bfloat16)
    value_proj = jnp.einsum('bsd,de->bse', act_full, w_value, preferred_element_type=jnp.float32).astype(jnp.bfloat16)
    cos_t, sin_t = rope_tables(positions, head_dim)
    cos_h = cos_t[:, :, None]
    sin_h = sin_t[:, :, None]
    q_rot = (apply_rope(query.astype(jnp.float32), cos_h, sin_h) * scale).astype(jnp.bfloat16)
    k_rot = apply_rope(key_proj.astype(jnp.float32), cos_t, sin_t).astype(jnp.bfloat16)
    scores = jnp.einsum('crie,cle->cirl', q_rot, k_rot, preferred_element_type=jnp.float32)
    causal = jnp.arange(seq_len)[:, None] >= jnp.arange(seq_len)[None, :]
    attn_probs = jax.nn.softmax(jnp.where(causal, scores, -1e30), axis=-1)
    probs_low = attn_probs.astype(jnp.bfloat16)
    attended = jnp.einsum('cirl,cle->crie', probs_low, value_proj, preferred_element_type=jnp.float32).astype(jnp.bfloat16).reshape(batch, seq_len, heads_dev * head_dim)
    out_part = jnp.einsum('bse,ed->bsd', attended, w_out, preferred_element_type=jnp.float32).astype(jnp.bfloat16)
    out_local = lax.psum_scatter(out_part, 'tp', scatter_dimension=1, tiled=True)
    output = (hidden_f + out_local.astype(jnp.float32)).astype(jnp.bfloat16)

    grad_full = lax.all_gather(grad_out, 'tp', axis=1, tiled=True)
    grad_w_out = jnp.einsum('bse,bsd->ed', attended, grad_full, preferred_element_type=jnp.float32)
    grad_att = jnp.einsum('bsd,ed->bse', grad_full, w_out, preferred_element_type=jnp.float32).astype(jnp.bfloat16).reshape(batch, seq_len, heads_dev, head_dim)
    grad_value = jnp.einsum('cirl,crie->cle', probs_low, grad_att, preferred_element_type=jnp.float32).astype(jnp.bfloat16)
    grad_probs = jnp.einsum('crie,cle->cirl', grad_att, value_proj, preferred_element_type=jnp.float32)
    row_dot = jnp.sum(grad_probs * attn_probs, axis=-1, keepdims=True)
    grad_scores = (attn_probs * (grad_probs - row_dot)).astype(jnp.bfloat16)
    grad_qrot = jnp.einsum('cirl,cle->crie', grad_scores, k_rot, preferred_element_type=jnp.float32)
    grad_krot = jnp.einsum('cirl,crie->cle', grad_scores, q_rot, preferred_element_type=jnp.float32)
    grad_query = apply_rope(grad_qrot * scale, cos_h, -sin_h).astype(jnp.bfloat16).reshape(batch, seq_len, heads_dev * head_dim)
    grad_key = apply_rope(grad_krot, cos_t, -sin_t).astype(jnp.bfloat16)
    grad_w_query = jnp.einsum('bsd,bse->de', act_full, grad_query, preferred_element_type=jnp.float32)
    grad_w_key = jnp.einsum('bsd,bse->de', act_full, grad_key, preferred_element_type=jnp.float32)
    grad_w_value = jnp.einsum('bsd,bse->de', act_full, grad_value, preferred_element_type=jnp.float32)
    grad_w_key, grad_w_value = lax.psum((grad_w_key, grad_w_value), 'tp')
    grad_act_part = (jnp.einsum('bse,de->bsd', grad_query, w_query, preferred_element_type=jnp.float32)
                     + jnp.einsum('bse,de->bsd', grad_key, w_key, preferred_element_type=jnp.float32)
                     + jnp.einsum('bse,de->bsd', grad_value, w_value, preferred_element_type=jnp.float32)).astype(jnp.bfloat16)
    grad_act = lax.psum_scatter(grad_act_part, 'tp', scatter_dimension=1, tiled=True).astype(jnp.float32)
    grad_norm_part = jnp.sum(grad_act * normed, axis=(0, 1))
    grad_normed = grad_act * gain
    grad_hidden = (grad_out.astype(jnp.float32) + inv_rms * (grad_normed - normed * jnp.mean(grad_normed * normed, axis=-1, keepdims=True))).astype(jnp.bfloat16)
    grad_norm_w = lax.psum(grad_norm_part, 'tp')
    return output, grad_hidden, grad_w_query, grad_w_out, grad_w_key, grad_w_value, grad_norm_w


def solution(mesh):
    specs_in = (P('dp', 'tp', None), P('dp', None), P(None), P(None, 'tp'), P(None, None), P(None, None), P('tp', None), P('dp', 'tp', None))
    specs_out = (P('dp', 'tp', None), P('dp', 'tp', None), P('dp', 'tp'), P(('dp', 'tp'), None), P('dp', None), P('dp', None), P('dp'))
    return jax.shard_map(local_block, mesh=mesh, in_specs=specs_in, out_specs=specs_out, check_vma=False)
```

profile of v0, /device:TPU:81, one launch (start us, length us, event | category | flops | bytes accessed | tf_op | source)
XLA Modules:
  0.0 374.8 jit_solution(683902995806245748)
XLA Ops:
  14.4 49.5 %all-gather.3.cloned.1.call-done = bf16[1,2048,2048]{2,1,0:T(8,128)(2,1)} async-done(((bf16[1,256,2048]{2,1,0:T(8,128)(2,1)}), bf16[1,2048,2048]{2,1,0:T(8,128)(2,1)}) %all-gather.3.cloned.1.call-update) | async-done | bytes 8388624 | tf_op jit(solution)/shard_map/all_gather | solution.py:32
  63.9 5.9 %fusion.65 = f32[1,2048,256]{1,2,0:T(8,128)S(1)} fusion(bf16[2048,256]{1,0:T(8,128)(2,1)S(1)} %copy-done, bf16[1,2048,2048]{2,1,0:T(8,128)(2,1)} %all-gather.3.cloned.1.call-done), kind=kOutput, calls=%fused_computation.58 | convolution fusion | flops 2148532224 | bytes 11534336 | tf_op jit(solution)/shard_map/bsd,de->bse/dot_general | solution.py:34
  69.8 4.7 %fusion.115 = (bf16[2048,128]{0,1:T(8,128)(2,1)S(1)}, bf16[2048,128]{0,1:T(8,128)(2,1)S(1)}) fusion(f32[1,2048,256]{1,2,0:T(8,128)S(1)} %fusion.65, f32[128]{0:T(128)S(1)} %multiply_power_fusion, f32[2048]{0:T(1024)S(1)} %bitcast.143), kind=kLoop, calls=%fused_computation.114 | loop fusion | flops 2359296 | bytes 3154432 | tf_op jit(solution)/shard_map/concatenate | solution.py:18
  81.1 7.3 %fusion.5 = (f32[2048]{0:T(1024)S(1)}, f32[2048,2048]{1,0:T(8,128)}) fusion(f32[2048,128]{0,1:T(8,128)S(1)} %get-tuple-element.16, f32[2048,128]{0,1:T(8,128)S(1)} %get-tuple-element.15, bf16[2048,128]{0,1:T(8,128)(2,1)S(1)} %get-tuple-element.18, bf16[2048,128]{0,1:T(8,128)(2,1)S(1)} %get-tuple-element.17), kind=kOutput, calls=%fused_computation.11 | convolution fusion | flops 2163734528 | bytes 19931136 | tf_op jit(solution)/shard_map/crie,cle->cirl/dot_general | solution.py:41
  88.4 7.3 %fusion.4 = f32[2048]{0:T(1024)S(1)} fusion(f32[2048,2048]{1,0:T(8,128)} %get-tuple-element.22, f32[2048]{0:T(1024)S(1)} %get-tuple-element.21), kind=kLoop, calls=%fused_computation.10 | loop fusion | flops 16775168 | bytes 16793600 | tf_op jit(solution)/shard_map/reduce_sum | solution.py:43
  95.7 16.4 %all-gather.5.cloned.1.call-done = bf16[1,2048,2048]{2,1,0:T(8,128)(2,1)} async-done(((bf16[1,256,2048]{2,1,0:T(8,128)(2,1)}), bf16[1,2048,2048]{2,1,0:T(8,128)(2,1)}) %all-gather.5.cloned.1.call-update) | async-done | bytes 8388624 | tf_op jit(solution)/shard_map/all_gather | solution.py:50
  112.1 6.2 %fusion.49 = bf16[2048,256]{1,0:T(8,128)(2,1)S(1)} fusion(bf16[256,2048]{1,0:T(8,128)(2,1)} %param.14, bf16[1,2048,2048]{2,1,0:T(8,128)(2,1)} %all-gather.5.cloned.1.call-done), kind=kOutput, calls=%fused_computation.52 | convolution fusion | flops 2148007936 | bytes 10485760 | tf_op jit(solution)/shard_map/bsd,ed->bse/dot_general | solution.py:52
  120.6 5.4 %fusion.46 = bf16[2048,256]{1,0:T(8,128)(2,1)} fusion(bf16[2048,256]{1,0:T(8,128)(2,1)S(1)} %fusion.49, f32[2048]{0:T(1024)S(1)} %fusion.4, f32[2048]{0:T(1024)S(1)} %get-tuple-element.21, f32[2048,2048]{1,0:T(8,128)S(1)} %copy-done.1), kind=kOutput, calls=%fused_computation.51 | convolution fusion | flops 2168979456 | bytes 18890752 | tf_op jit(solution)/shard_map/cirl,crie->cle/dot_general | solution.py:53
  129.4 10.8 %fusion = (f32[2048]{0:T(1024)}, f32[2048,2048]{1,0:T(8,128)}) fusion(f32[2048]{0:T(1024)S(1)} %fusion.4, f32[2048]{0:T(1024)S(1)} %get-tuple-element.21, f32[2048,2048]{1,0:T(8,128)S(1)} %copy-done.1, bf16[2048,256]{1,0:T(8,128)(2,1)} %fusion.34, bf16[2048,256]{1,0:T(8,128)(2,1)} %copy-done.22), kind=kOutput, calls=%fused_computation.3 | convolution fusion | flops 2172647424 | bytes 35676160 | tf_op jit(solution)/shard_map/crie,cle->cirl/dot_general | solution.py:54
  140.2 8.9 %fusion.6 = bf16[2048,2048]{0,1:T(8,128)(2,1)S(1)} fusion(f32[2048,2048]{1,0:T(8,128)} %get-tuple-element.24, f32[2048]{0:T(1024)} %get-tuple-element.23, f32[2048]{0:T(1024)S(1)} %fusion.4, f32[2048]{0:T(1024)S(1)} %get-tuple-element.21, f32[2048,2048]{1,0:T(8,128)S(1)} %copy-done.1), kind=kLoop, calls=%fused_computation.12 | loop fusion | flops 29360128 | bytes 41967616 | tf_op jit(solution)/shard_map/reshape.39
  154.0 4.3 %fusion.119 = (bf16[2048,128]{0,1:T(8,128)(2,1)S(1)}, bf16[2048,128]{0,1:T(8,128)(2,1)S(1)}) fusion(f32[1,2048,1,256]{1,3,2,0:T(8,128)S(1)} %fusion.33, f32[128]{0:T(128)S(1)} %copy-done.20, f32[2048]{0:T(1024)S(1)} %bitcast.145), kind=kLoop, calls=%fused_computation.118 | loop fusion | flops 2621440 | bytes 3154432 | tf_op jit(solution)/shard_map/concatenate | solution.py:18
  158.3 4.5 %fusion.117 = (bf16[2048,128]{0,1:T(8,128)(2,1)S(1)}, bf16[2048,128]{0,1:T(8,128)(2,1)S(1)}) fusion(f32[1,2048,256]{1,2,0:T(8,128)S(1)} %convolution_bitcast_fusion, f32[128]{0:T(128)S(1)} %copy-done.20, f32[2048]{0:T(1024)S(1)} %bitcast.146), kind=kLoop, calls=%fused_computation.116 | loop fusion | flops 2621440 | bytes 3154432 | tf_op jit(solution)/shard_map/concatenate | solution.py:18
  162.7 8.1 %fusion.111 = f32[2048,2048]{1,0:T(8,128)} fusion(bf16[2048,256]{1,0:T(8,128)(2,1)S(1)} %copy-done, bf16[2048,128]{0,1:T(8,128)(2,1)S(1)} %get-tuple-element.12, bf16[2048,128]{0,1:T(8,128)(2,1)S(1)} %get-tuple-element.11), kind=kOutput, calls=%fused_computation.110 | convolution fusion | flops 2149580800 | bytes 18874368 | tf_op jit(solution)/shard_map/bse,de->bsd/dot_general | solution.py:66
  170.9 8.2 %fusion.112 = f32[2048,2048]{1,0:T(8,128)} fusion(bf16[2048,256]{1,0:T(8,128)(2,1)S(1)} %copy-done.7, bf16[2048,128]{0,1:T(8,128)(2,1)S(1)} %get-tuple-element.14, bf16[2048,128]{0,1:T(8,128)(2,1)S(1)} %get-tuple-element.13), kind=kOutput, calls=%fused_computation.111 | convolution fusion | flops 2149580800 | bytes 18874368 | tf_op jit(solution)/shard_map/bse,de->bsd/dot_general | solution.py:65
  179.1 15.0 %fusion.28 = bf16[1,2048,2048]{2,1,0:T(8,128)(2,1)} fusion(bf16[2048,256]{1,0:T(8,128)(2,1)} %fusion.46, bf16[2048,256]{1,0:T(8,128)(2,1)} %param.13, f32[2048,2048]{1,0:T(8,128)} %fusion.112, f32[2048,2048]{1,0:T(8,128)} %fusion.111), kind=kOutput, calls=%fused_computation.35 | convolution fusion | flops 2160066560 | bytes 44040192 | tf_op jit(solution)/shard_map/bse,de->bsd/dot_general | solution.py:67
  194.2 9.0 %fusion.53 = bf16[2048,256]{0,1:T(8,128)(2,1)S(1)} fusion(bf16[2048,256]{1,0:T(8,128)(2,1)} %fusion.34, f32[2048]{0:T(1024)S(1)} %fusion.4, f32[2048]{0:T(1024)S(1)} %get-tuple-element.21, f32[2048,2048]{1,0:T(8,128)} %get-tuple-element.22), kind=kOutput, calls=%fused_computation.54 | convolution fusion | flops 2168979456 | bytes 18890752 | tf_op jit(solution)/shard_map/cirl,cle->crie/dot_general | solution.py:45
  204.2 5.6 %convert_bitcast_fusion = bf16[1,2048,2048]{2,1,0:T(8,128)(2,1)} fusion(bf16[2048,256]{0,1:T(8,128)(2,1)S(1)} %fusion.53, bf16[256,2048]{1,0:T(8,128)(2,1)S(1)} %copy-done.12), kind=kOutput, calls=%fused_computation.33 | convolution fusion | flops 2151677952 | bytes 10485760 | tf_op jit(solution)/shard_map/bse,ed->bsd/dot_general | solution.py:46
  210.3 7.3 %fusion.17 = f32[2048,256]{1,0:T(8,128)} fusion(bf16[1,2048,2048]{2,1,0:T(8,128)(2,1)} %all-gather.3.cloned.1.call-done, bf16[2048,128]{0,1:T(8,128)(2,1)S(1)} %get-tuple-element.12, bf16[2048,128]{0,1:T(8,128)(2,1)S(1)} %get-tuple-element.11), kind=kOutput, calls=%fused_computation.23 | convolution fusion | flops 2149580800 | bytes 11534336 | tf_op jit(solution)/shard_map/bsd,bse->de/dot_general | solution.py:62
  217.5 7.2 %fusion.15 = f32[2048,256]{1,0:T(8,128)} fusion(bf16[2048,256]{1,0:T(8,128)(2,1)S(1)} %copy-done.9, bf16[1,2048,2048]{2,1,0:T(8,128)(2,1)} %all-gather.3.cloned.1.call-done), kind=kOutput, calls=%fused_computation.21 | convolution fusion | flops 2147483648 | bytes 11534336 | tf_op jit(solution)/shard_map/bsd,bse->de/dot_general | solution.py:63
  224.8 7.3 %fusion.19 = f32[2048,256]{1,0:T(8,128)} fusion(bf16[1,2048,2048]{2,1,0:T(8,128)(2,1)} %all-gather.3.cloned.1.call-done, bf16[2048,128]{0,1:T(8,128)(2,1)S(1)} %get-tuple-element.14, bf16[2048,128]{0,1:T(8,128)(2,1)S(1)} %get-tuple-element.13), kind=kOutput, calls=%fused_computation.25 | convolution fusion | flops 2149580800 | bytes 11534336 | tf_op jit(solution)/shard_map/bsd,bse->de/dot_general | solution.py:61
  232.1 7.2 %fusion.7 = f32[256,2048]{1,0:T(8,128)} fusion(bf16[2048,256]{0,1:T(8,128)(2,1)S(1)} %copy-done.5, bf16[1,2048,2048]{2,1,0:T(8,128)(2,1)} %all-gather.5.cloned.1.call-done), kind=kOutput, calls=%fused_computation.13 | convolution fusion | flops 2147483648 | bytes 11534336 | tf_op jit(solution)/shard_map/bse,bsd->ed/dot_general | solution.py:51
  245.1 13.9 %psum.23 = f32[2048]{0:T(1024)} all-reduce(f32[2048]{0:T(1024)S(1)} %get-tuple-element.7), channel_id=1, replica_groups=mesh['dp'=4,'tp'=8] {'tp'}, use_global_device_ids=true, to_apply=%region_10.11 | all-reduce | flops 2048 | bytes 16384 | tf_op jit(solution)/shard_map/psum | solution.py:72
  259.0 35.4 %reduce-scatter.3.cloned.1.call-done = bf16[1,256,2048]{2,1,0:T(8,128)(2,1)} async-done(((bf16[1,2048,2048]{2,1,0:T(8,128)(2,1)}), bf16[1,256,2048]{2,1,0:T(8,128)(2,1)}) %reduce-scatter.3.cloned.1.call-update) | async-done | bytes 1048592 | tf_op jit(solution)/shard_map/reduce_scatter | solution.py:47
  298.3 63.4 %all-reduce.3.cloned.1.call-done = (f32[2048,256]{1,0:T(8,128)}, f32[2048,256]{1,0:T(8,128)}) async-done(((f32[2048,256]{1,0:T(8,128)}, f32[2048,256]{1,0:T(8,128)}), (f32[2048,256]{1,0:T(8,128)}, f32[2048,256]{1,0:T(8,128)})) %all-reduce.3.cloned.1.call-update) | async-done | bytes 4194320 | tf_op jit(solution)/shard_map/psum | solution.py:64
  (78 shorter events, 41.7 us)
Async XLA Ops:
  7.2 56.7 %copy-start = (bf16[2048,256]{1,0:T(8,128)(2,1)S(1)}, bf16[2048,256]{1,0:T(8,128)(2,1)}, u32[]{:S(2)}) copy-start(bf16[2048,256]{1,0:T(8,128)(2,1)} %param.12) | copy-start | bytes 3145732
  7.2 56.7 %all-gather.3.cloned.1.call-start = ((), (), s32[]{:S(2)}) async-start(), calls=%async_computation.2 | async-start | bytes 9437184 | tf_op jit(solution)/shard_map/all_gather | solution.py:32
  12.7 99.4 %all-gather.5.cloned.1.call-start = ((), (), s32[]{:S(2)}) async-start(), calls=%async_computation.4 | async-start | bytes 9437184 | tf_op jit(solution)/shard_map/all_gather | solution.py:50
  13.5 229.5 %reduce-scatter.5.cloned.1.call-start = ((), (), s32[]{:S(2)}) async-start(), calls=%async_computation.5 | async-start | bytes 9437184 | tf_op jit(solution)/shard_map/reduce_scatter | solution.py:68
  14.3 62.5 %copy-start.19 = (f32[128]{0:T(128)}, f32[128]{0:T(128)S(1)}, u32[]{:S(2)}) copy-start(f32[128]{0:T(128)S(1)} %multiply_power_fusion) | copy-start | bytes 1540
  14.3 60.1 %copy-start.6 = (bf16[2048,256]{1,0:T(8,128)(2,1)S(1)}, bf16[2048,256]{1,0:T(8,128)(2,1)}, u32[]{:S(2)}) copy-start(bf16[2048,256]{1,0:T(8,128)(2,1)} %param.11) | copy-start | bytes 3145732
  63.9 10.6 %copy-start.21 = (bf16[1,2048,2048]{2,1,0:T(8,128)(2,1)S(1)}, bf16[1,2048,2048]{2,1,0:T(8,128)(2,1)}, u32[]{:S(2)}) copy-start(bf16[1,2048,2048]{2,1,0:T(8,128)(2,1)} %all-gather.3.cloned.1.call-done) | copy-start | bytes 25165828
  74.5 6.6 %copy-start.13 = (bf16[2048,128]{0,1:T(8,128)(2,1)}, bf16[2048,128]{0,1:T(8,128)(2,1)S(1)}, u32[]{:S(2)}) copy-start(bf16[2048,128]{0,1:T(8,128)(2,1)S(1)} %get-tuple-element.18) | copy-start | bytes 1572868
  81.1 7.3 %copy-start.10 = (f32[2048,128]{0,1:T(8,128)}, f32[2048,128]{0,1:T(8,128)S(1)}, u32[]{:S(2)}) copy-start(f32[2048,128]{0,1:T(8,128)S(1)} %get-tuple-element.16) | copy-start | bytes 3145732
  112.1 8.5 %copy-start.1 = (f32[2048,2048]{1,0:T(8,128)S(1)}, f32[2048,2048]{1,0:T(8,128)}, u32[]{:S(2)}) copy-start(f32[2048,2048]{1,0:T(8,128)} %get-tuple-element.22) | copy-start | bytes 50331652
  112.1 13.8 %slice-start = ((s8[8388608]{0:T(1024)(128)(4,1)}), s8[4194304]{0:T(1024)(128)(4,1)S(1)}, s32[]{:S(2)}) async-start(s8[8388608]{0:T(1024)(128)(4,1)} %bitcast.147), calls=%async_computation.7 | async-start | bytes 8388608
  120.6 5.4 %copy-start.8 = (bf16[2048,256]{1,0:T(8,128)(2,1)S(1)}, bf16[2048,256]{1,0:T(8,128)(2,1)}, u32[]{:S(2)}) copy-start(bf16[2048,256]{1,0:T(8,128)(2,1)} %param.13) | copy-start | bytes 3145732
  120.6 5.4 %slice-start.1 = ((s8[8388608]{0:T(1024)(128)(4,1)}), s8[4194304]{0:T(1024)(128)(4,1)S(1)}, s32[]{:S(2)}) async-start(s8[8388608]{0:T(1024)(128)(4,1)} %bitcast.147), calls=%async_computation.8 | async-start | bytes 8388608
  140.2 8.9 %copy-start.11 = (f32[2048,128]{0,1:T(8,128)S(1)}, f32[2048,128]{0,1:T(8,128)}, u32[]{:S(2)}) copy-start(f32[2048,128]{0,1:T(8,128)} %copy-done.10) | copy-start | bytes 3145732
  162.7 8.2 %copy-start.7 = (bf16[2048,256]{1,0:T(8,128)(2,1)S(1)}, bf16[2048,256]{1,0:T(8,128)(2,1)}, u32[]{:S(2)}) copy-start(bf16[2048,256]{1,0:T(8,128)(2,1)} %param.11) | copy-start | bytes 3145732
  194.1 100.3 %reduce-scatter.3.cloned.1.call-start = ((), (), s32[]{:S(2)}) async-start(), calls=%async_computation.3 | async-start | bytes 9437184 | tf_op jit(solution)/shard_map/reduce_scatter | solution.py:47
  194.2 10.0 %copy-start.12 = (bf16[256,2048]{1,0:T(8,128)(2,1)S(1)}, bf16[256,2048]{1,0:T(8,128)(2,1)}, u32[]{:S(2)}) copy-start(bf16[256,2048]{1,0:T(8,128)(2,1)} %param.14) | copy-start | bytes 3145732
  209.9 151.8 %all-reduce.3.cloned.1.call-start = ((), (), s32[]{:S(2)}) async-start(), calls=%async_computation.6 | async-start | bytes 8388608 | tf_op jit(solution)/shard_map/psum | solution.py:64
  210.2 7.3 %copy-start.9 = (bf16[2048,256]{1,0:T(8,128)(2,1)S(1)}, bf16[2048,256]{1,0:T(8,128)(2,1)}, u32[]{:S(2)}) copy-start(bf16[2048,256]{1,0:T(8,128)(2,1)} %fusion.46) | copy-start | bytes 3145732
  224.8 7.3 %copy-start.5 = (bf16[2048,256]{0,1:T(8,128)(2,1)S(1)}, bf16[2048,256]{0,1:T(8,128)(2,1)}, u32[]{:S(2)}) copy-start(bf16[2048,256]{0,1:T(8,128)(2,1)} %copy-done.4) | copy-start | bytes 3145732
  232.1 11.0 %copy-start.2 = (bf16[1,256,2048]{2,1,0:T(8,128)(2,1)S(1)}, bf16[1,256,2048]{2,1,0:T(8,128)(2,1)}, u32[]{:S(2)}) copy-start(bf16[1,256,2048]{2,1,0:T(8,128)(2,1)} %param.8) | copy-start | bytes 3145732
  232.1 11.0 %copy-start.16 = (f32[2048]{0:T(1024)S(1)}, f32[2048]{0:T(1024)}, u32[]{:S(2)}) copy-start(f32[2048]{0:T(1024)} %copy-done.15) | copy-start | bytes 24580
  232.1 11.0 %copy-start.18 = (f32[256]{0:T(256)S(1)}, f32[256]{0:T(256)}, u32[]{:S(2)}) copy-start(f32[256]{0:T(256)} %copy-done.17) | copy-start | bytes 3076
  232.1 62.3 %copy-start.3 = (bf16[1,256,2048]{2,1,0:T(8,128)(2,1)S(1)}, bf16[1,256,2048]{2,1,0:T(8,128)(2,1)}, u32[]{:S(2)}) copy-start(bf16[1,256,2048]{2,1,0:T(8,128)(2,1)} %param.15) | copy-start | bytes 3145732
  (6 other events, 12.5 us)
Sparse Core Ops, SparseCore 0:
  12.9 50.9 all-gather.2
  65.5 46.6 all-gather.4
  194.2 48.7 reduce-scatter.4
  245.2 49.1 reduce-scatter.2
  297.3 64.4 all-reduce.2
where the time goes:
time: 379 us; the launch traced here: 375 us
  waiting for transfers between devices  169 us (45%)
  matrix products  121 us (32%)
  other arithmetic  45.4 us (12%)
  between operations  14.6 us (4%)
  blocking collectives  13.9 us (4%)
  local copies, waits for them, and re-layouts  10.1 us (3%)
    psum x1, waiting for transfers between devices, local_block(): grad_w_key, grad_w_value = lax.psum((grad_w_key, grad_w_value), 'tp')  63.4 us
    all_gather x1, waiting for transfers between devices, local_block(): act_full = lax.all_gather(act_local, 'tp', axis=1, tiled=True)  49.5 us
    reduce_scatter x1, waiting for transfers between devices, local_block(): lax.psum_scatter(out_part, 'tp', scatter_dimension=1, tiled=True)  35.4 us
    concatenate x4, other arithmetic, apply_rope(): jnp.concatenate([first * cos_t - second * sin_t, second * cos_t + first *...  17.6 us
    all_gather x1, waiting for transfers between devices, local_block(): grad_full = lax.all_gather(grad_out, 'tp', axis=1, tiled=True)  16.4 us
    dot_general x1, matrix products, local_block(): jnp.einsum('bse,de->bsd', grad_value, w_value, preferred_element_type=jnp...  15 us
    psum x1, blocking collectives, local_block(): grad_norm_w = lax.psum(grad_norm_part, 'tp')  13.9 us
    dot_general x1, matrix products, local_block(): jnp.einsum('crie,cle->cirl', grad_att, value_proj, preferred_element_type...  10.8 us
  transfers between devices with their start and end apart: 5, of which 5 were waited for; matrix products, arithmetic and copies ran while one was open for 22% of the time, Pallas kernels for 0%

commit v1 on v0

v1 whole, which is shorter than its diff:
```python
import functools

import jax
import jax.numpy as jnp
from jax import lax
from jax.experimental import pallas as pl
from jax.experimental.pallas import tpu as pltpu
from jax.sharding import PartitionSpec as P

MESH = pl.DeviceIdType.MESH
F32 = jnp.float32
BF16 = jnp.bfloat16
TILE = 512
COLS = 512
VMEM_LIMIT = 63 * 1024 * 1024


def dot_nn(a, b):
    return lax.dot_general(a, b, (((1,), (0,)), ((), ())), preferred_element_type=F32)


def dot_nt(a, b):
    return lax.dot_general(a, b, (((1,), (1,)), ((), ())), preferred_element_type=F32)


def dot_tn(a, b):
    return lax.dot_general(a, b, (((0,), (0,)), ((), ())), preferred_element_type=F32)


def rope(u, cos_t, sin_t):
    half = u.shape[-1] // 2
    first, second = u[:, :half], u[:, half:]
    return jnp.concatenate([first * cos_t - second * sin_t, second * cos_t + first * sin_t], axis=-1)


class Place:
    def __init__(self, size):
        n = size // 2
        self.me = lax.axis_index('tp')
        self.core = lax.rem(self.me, 2)
        self.chip = lax.div(self.me, 2)
        self.chip_r = lax.rem(self.chip + 1, n)
        self.chip_l = lax.rem(self.chip + n - 1, n)
        self.chip_o = lax.rem(self.chip + 2, n)
        self.right = self.chip_r * 2 + self.core
        self.left = self.chip_l * 2 + self.core
        self.sib = self.chip * 2 + 1 - self.core


def remote(src, dst, ssem, rsem, to):
    return pltpu.make_async_remote_copy(src_ref=src, dst_ref=dst, send_sem=ssem, recv_sem=rsem,
                                        device_id={'tp': to}, device_id_type=MESH)


def rows_of(start, size):
    return pl.ds(pl.multiple_of(start, min(size, 128)), size)


class Gather:
    def __init__(self, place, full, block, ssem, rsem):
        self.p, self.full, self.block, self.ssem, self.rsem = place, full, block, ssem, rsem
        p = place
        half = block // 2
        regions = []
        for core in (p.core, 1 - p.core):
            for chip in (p.chip_l, p.chip_r, p.chip_o):
                for h in (0, 1):
                    regions.append(rows_of((chip * 2 + core) * block + h * half, half))
        own_other = rows_of(p.sib * block, block)
        self.regions = regions[:6] + [own_other] + regions[6:]
        self.own = [rows_of(p.me * block + h * half, half) for h in (0, 1)]
        self.own_all = rows_of(p.me * block, block)

    def _send(self, sem, src, rows, rsem, to):
        copy = remote(src, self.full.at[rows], self.ssem.at[sem], self.rsem.at[rsem], to)
        copy.start()

    def start(self, src=None):
        p, half = self.p, self.block // 2
        parts = [self.full.at[r] for r in self.own] if src is None else [src.at[pl.ds(h * half, half)] for h in (0, 1)]
        whole = self.full.at[self.own_all] if src is None else src
        self._send(0, parts[0], self.own[0], 0, p.right)
        self._send(3, parts[1], self.own[1], 3, p.left)
        self._send(1, parts[1], self.own[1], 1, p.right)
        self._send(2, parts[0], self.own[0], 2, p.left)
        self._send(6, whole, self.own_all, 6, p.sib)

    def recv(self, *which):
        for k in which:
            ref = self.full.at[self.regions[k]]
            remote(ref, ref, self.ssem.at[k], self.rsem.at[k], self.p.sib).wait_recv()

    def relay(self):
        self._send(4, self.full.at[self.regions[0]], self.regions[0], 4, self.p.right)
        self._send(5, self.full.at[self.regions[3]], self.regions[3], 5, self.p.left)

    def forward(self, *which):
        for k in which:
            self._send(7 + k, self.full.at[self.regions[k]], self.regions[k], 7 + k, self.p.sib)

    def finish(self):
        for k in range(13):
            ref = self.full.at[self.own_all if k == 6 else self.own[0]]
            remote(ref, ref, self.ssem.at[k], self.rsem.at[k], self.p.sib).wait_send()


class Scatter:
    def __init__(self, place, block, width, tile, dtype, prod, d2d, sums, top, bot, from_l, from_r, ssem, rsem,
                 stage=None, source=None):
        self.__dict__.update(locals())
        self.half = block // 2

    def row(self, chip, core, h=0):
        return (chip * 2 + core) * self.block + h * self.half

    def tiles(self, fn):
        if self.width == self.tile:
            fn(pl.ds(0, self.width))
        else:
            @pl.loop(0, self.width // self.tile)
            def _(n):
                fn(pl.ds(pl.multiple_of(n * self.tile, self.tile), self.tile))

    def chip_send(self):
        p = self.place
        for k, chip in enumerate((p.chip_o, p.chip_r, p.chip_l, p.chip)):
            row = self.row(chip, 1 - p.core)
            if self.source is None:
                slot = k % 2
                if k >= 2:
                    ref = self.stage.at[slot]
                    remote(ref, ref, self.ssem.at[k - 2], self.rsem.at[0], p.sib).wait_send()

                def fill(cols, row=row, slot=slot):
                    self.stage[slot, :, cols] = self.prod(row, self.block, cols).astype(self.dtype)
                self.tiles(fill)
                src = self.stage.at[slot]
            else:
                src = self.source.at[rows_of(row, self.block)]
            remote(src, self.d2d.at[k], self.ssem.at[k], self.rsem.at[k], p.sib).start()

    def chip_recv(self, k):
        ref = self.d2d.at[k]
        remote(ref, ref, self.ssem.at[k], self.rsem.at[k], self.place.sib).wait_recv()

    def far(self):
        p, half = self.place, self.half
        self.chip_recv(0)

        def fill(cols):
            total = self.prod(self.row(p.chip_o, p.core), self.block, cols) + self.d2d[0, :, cols].astype(F32)
            self.sums[0, :, cols] = total.astype(self.dtype)
        self.tiles(fill)
        remote(self.sums.at[0, pl.ds(0, half)], self.top, self.ssem.at[4], self.rsem.at[4], p.right).start()
        remote(self.sums.at[0, pl.ds(half, half)], self.bot, self.ssem.at[5], self.rsem.at[5], p.left).start()

    def near_half(self, k, h, chip, extra, dst, sem, to):
        half = self.half
        rows = pl.ds(h * half, half)

        def fill(cols):
            total = self.prod(self.row(chip, self.place.core, h), half, cols) + self.d2d[k, rows, cols].astype(F32)
            if extra is not None:
                total = total + extra[:, cols].astype(F32)
            self.sums[k, rows, cols] = total.astype(self.dtype)
        self.tiles(fill)
        remote(self.sums.at[k, rows], dst.at[rows], self.ssem.at[sem], self.rsem.at[sem], to).start()

    def near_first(self):
        p = self.place
        self.chip_recv(1)
        self.near_half(1, 1, p.chip_r, None, self.from_l, 6, p.right)
        self.chip_recv(2)
        self.near_half(2, 0, p.chip_l, None, self.from_r, 8, p.left)

    def near_second(self):
        p = self.place
        remote(self.top, self.top, self.ssem.at[4], self.rsem.at[4], p.right).wait_recv()
        self.near_half(1, 0, p.chip_r, self.top, self.from_l, 7, p.right)
        remote(self.bot, self.bot, self.ssem.at[5], self.rsem.at[5], p.left).wait_recv()
        self.near_half(2, 1, p.chip_l, self.bot, self.from_r, 9, p.left)

    def last(self, fn):
        p, half = self.place, self.half
        self.chip_recv(3)
        for sem, ref, h in ((6, self.from_l, 1), (7, self.from_l, 0), (8, self.from_r, 0), (9, self.from_r, 1)):
            part = ref.at[pl.ds(h * half, half)]
            remote(part, part, self.ssem.at[sem], self.rsem.at[sem], p.sib).wait_recv()

        def fill(cols):
            total = self.prod(self.row(p.chip, p.core), self.block, cols) + self.d2d[3, :, cols].astype(F32)
            fn(cols, total + self.from_l[:, cols].astype(F32) + self.from_r[:, cols].astype(F32))
        self.tiles(fill)

    def chip_done(self):
        for k in (range(4) if self.source is not None else (2, 3)):
            ref = self.d2d.at[k]
            remote(ref, ref, self.ssem.at[k], self.rsem.at[k], self.place.sib).wait_send()

    def ring_done(self):
        for k in range(4, 10):
            remote(self.top, self.top, self.ssem.at[k], self.rsem.at[k], self.place.sib).wait_send()


def gather_kernel(size, x_ref, dout_ref, gain_ref, angle_ref, wq_hbm, wk_hbm, wv_hbm,
                  a_out, dout_out, q_ref, k_ref, v_ref, o_ref, lse_ref, cos_ref, sin_ref,
                  a_full, wbuf, s_scr, m_scr, l_scr, acc_scr, lsem, ssem_a, rsem_a, ssem_d, rsem_d):
    p = Place(size)
    block = x_ref.shape[0]
    seq, head = q_ref.shape
    scale = head ** -0.5
    weights = [pltpu.make_async_copy(w, wbuf.at[i], lsem.at[i]) for i, w in enumerate((wq_hbm, wk_hbm, wv_hbm))]
    for w in weights:
        w.start()
    act = Gather(p, a_full, block, ssem_a, rsem_a)
    grad = Gather(p, dout_out, block, ssem_d, rsem_d)
    own_grad = pltpu.make_async_copy(dout_ref, dout_out.at[grad.own_all], lsem.at[3])
    own_grad.start()

    barrier = pltpu.get_barrier_semaphore()
    for peer in (p.left, p.right, p.sib):
        pl.semaphore_signal(barrier, inc=1, device_id={'tp': peer}, device_id_type=MESH)

    @pl.loop(0, block // 64)
    def _(n):
        rows = pl.ds(pl.multiple_of(n * 64, 64), 64)
        x_f = x_ref[rows, :].astype(F32)
        inv = lax.rsqrt(jnp.mean(x_f * x_f, axis=-1, keepdims=True) + 1e-6)
        a_full[rows_of(p.me * block + n * 64, 64), :] = (x_f * inv * gain_ref[...]).astype(BF16)

    pl.semaphore_wait(barrier, 3)
    act.start()

    @pl.loop(0, seq // 64)
    def _(n):
        rows = pl.ds(pl.multiple_of(n * 64, 64), 64)
        angle = angle_ref[rows, :]
        cos_ref[rows, :] = jnp.cos(angle)
        sin_ref[rows, :] = jnp.sin(angle)

    for w in weights:
        w.wait()

    def project(first, second):
        @pl.loop(0, 2)
        def _(n):
            rows = rows_of((first + n * (second - first)) * block, block)
            a = a_full[rows, :]
            cos_t, sin_t = cos_ref[rows, :], sin_ref[rows, :]
            query = dot_nn(a, wbuf[0]).astype(BF16).astype(F32)
            q_ref[rows, :] = (rope(query, cos_t, sin_t) * scale).astype(BF16)
            key = dot_nn(a, wbuf[1]).astype(BF16).astype(F32)
            k_ref[rows, :] = rope(key, cos_t, sin_t).astype(BF16)
            v_ref[rows, :] = dot_nn(a, wbuf[2]).astype(BF16)

    act.recv(6)
    project(p.me, p.sib)
    act.recv(0, 3)
    act.relay()
    grad.start(dout_ref)
    act.forward(0, 3)
    act.recv(1, 2)
    act.forward(1, 2)
    project(p.left, p.right)
    act.recv(7, 8, 9, 10)
    project(p.chip_l * 2 + 1 - p.core, p.chip_r * 2 + 1 - p.core)
    act.recv(4, 5)
    act.forward(4, 5)
    act.recv(11, 12)
    project(p.chip_o * 2 + p.core, p.chip_o * 2 + 1 - p.core)
    a_copy = pltpu.make_async_copy(a_full, a_out, lsem.at[4])
    a_copy.start()
    grad.recv(0, 3)
    grad.relay()
    grad.forward(0, 3)

    row_ids = lax.broadcasted_iota(jnp.int32, (TILE, TILE), 0)
    col_ids = lax.broadcasted_iota(jnp.int32, (TILE, TILE), 1)

    @pl.loop(0, seq // TILE)
    def _(i):
        rows = pl.ds(pl.multiple_of(i * TILE, TILE), TILE)
        m_scr[...] = jnp.full(m_scr.shape, -1e30, F32)
        l_scr[...] = jnp.zeros(l_scr.shape, F32)
        acc_scr[...] = jnp.zeros(acc_scr.shape, F32)

        @pl.loop(0, i + 1)
        def _(j):
            cols = pl.ds(pl.multiple_of(j * TILE, TILE), TILE)
            s = dot_nt(q_ref[rows, :], k_ref[cols, :])
            s = jnp.where(row_ids + (i - j) * TILE >= col_ids, s, -1e30)
            s_scr[j] = s
            m_old = m_scr[:, :1]
            m_new = jnp.maximum(m_old, jnp.max(s, axis=-1, keepdims=True))
            l_new = l_scr[:, :1] * jnp.exp(m_old - m_new) + jnp.sum(jnp.exp(s - m_new), axis=-1, keepdims=True)
            m_scr[...] = jnp.broadcast_to(m_new, m_scr.shape)
            l_scr[...] = jnp.broadcast_to(l_new, l_scr.shape)

        lse = m_scr[...] + jnp.log(l_scr[...])
        lse_ref[rows, :] = lse

        @pl.loop(0, i + 1)
        def _(j):
            cols = pl.ds(pl.multiple_of(j * TILE, TILE), TILE)
            prob = jnp.exp(s_scr[j] - lse_ref[rows, :1]).astype(BF16)
            acc_scr[...] += dot_nn(prob, v_ref[cols, :])

        o_ref[rows, :] = acc_scr[...].astype(BF16)

    grad.recv(1, 2)
    grad.forward(1, 2)
    grad.recv(4, 5)
    grad.forward(4, 5)
    grad.recv(6, 7, 8, 9, 10, 11, 12)
    act.finish()
    grad.finish()
    own_grad.wait()
    a_copy.wait()


def reduce_kernel(size, x_ref, dout_ref, gain_ref, q_ref, k_ref, v_ref, o_ref, lse_ref, cos_ref, sin_ref,
                  wo_ref, wq_ref, wk_ref, wv_ref, a_hbm, grad_hbm,
                  out_ref, dx_ref, dwq_out, dwo_out, dwk_out, dwv_out, dw_ref,
                  big, dq_ref, dkv_ref, dkv_full, dq_acc, stage, sums, d2d_a, top_a, bot_a, fl_a, fr_a,
                  d2d_b, top_b, bot_b, fl_b, fr_b, d2d_c, sums_c, top_c, bot_c, fl_c, fr_c,
                  wide, tiles, dw_me, dw_all, lsem, tsem, ss_a, rs_a, ss_b, rs_b, ss_c, rs_c, ss_g, rs_g, ss_w, rs_w):
    p = Place(size)
    block, width = x_ref.shape
    seq, head = q_ref.shape
    scale = head ** -0.5
    load_grad = pltpu.make_async_copy(grad_hbm, big, lsem.at[0])
    load_grad.start()

    barrier = pltpu.get_barrier_semaphore()
    peers = [lax.rem(p.me + d, size) for d in range(1, size)]
    for peer in peers:
        pl.semaphore_signal(barrier, inc=1, device_id={'tp': peer}, device_id_type=MESH)
    pl.semaphore_wait(barrier, size - 1)

    out_rs = Scatter(p, block, width, COLS, BF16,
                     lambda row, n, cols: dot_nn(o_ref[rows_of(row, n), :], wo_ref[:, cols]),
                     d2d_a, sums, top_a, bot_a, fl_a, fr_a, ss_a, rs_a, stage=stage)
    da_rs = Scatter(p, block, width, COLS, BF16,
                    lambda row, n, cols: dot_nt(dq_ref[rows_of(row, n), :], wq_ref[cols, :]),
                    d2d_b, sums, top_b, bot_b, fl_b, fr_b, ss_b, rs_b, stage=stage)
    kv_rs = Scatter(p, block, 2 * head, 2 * head, F32,
                    lambda row, n, cols: dkv_ref[rows_of(row, n), cols],
                    d2d_c, sums_c, top_c, bot_c, fl_c, fr_c, ss_c, rs_c, source=dkv_ref)
    kv_ag = Gather(p, dkv_full, block, ss_g, rs_g)

    out_rs.chip_send()
    out_rs.far()
    out_rs.near_first()
    out_rs.chip_done()
    dkv_ref[...] = jnp.zeros(dkv_ref.shape, F32)
    load_grad.wait()

    row_ids = lax.broadcasted_iota(jnp.int32, (TILE, TILE), 0)
    col_ids = lax.broadcasted_iota(jnp.int32, (TILE, TILE), 1)

    def backward(lo, hi):
        @pl.loop(lo, hi)
        def _(i):
            rows = pl.ds(pl.multiple_of(i * TILE, TILE), TILE)
            do_f = dot_nt(big[rows, :], wo_ref[...])
            do = do_f.astype(BF16)
            row_dot = jnp.sum(do.astype(F32) * o_ref[rows, :].astype(F32), axis=-1, keepdims=True)
            dq_acc[...] = jnp.zeros(dq_acc.shape, F32)
            q = q_ref[rows, :]

            @pl.loop(0, i + 1)
            def _(j):
                cols = pl.ds(pl.multiple_of(j * TILE, TILE), TILE)
                s = dot_nt(q, k_ref[cols, :])
                prob = jnp.exp(s - lse_ref[rows, :1])
                prob = jnp.where(row_ids + (i - j) * TILE >= col_ids, prob, 0.0)
                dkv_ref[cols, head:] += dot_tn(prob.astype(BF16), do)
                dprob = dot_nt(do, v_ref[cols, :])
                ds = (prob * (dprob - row_dot)).astype(BF16)
                dkv_ref[cols, :head] += dot_tn(ds, q)
                dq_acc[...] += dot_nn(ds, k_ref[cols, :])

            dq_ref[rows, :] = rope(dq_acc[...] * scale, cos_ref[rows, :], -sin_ref[rows, :]).astype(BF16)

    steps = seq // TILE
    backward(0, steps // 2)
    out_rs.near_second()
    backward(steps // 2, steps)

    kv_rs.chip_send()
    da_rs.chip_send()
    kv_rs.far()
    kv_rs.near_first()
    out_rs.ring_done()
    da_rs.far()
    da_rs.near_first()

    @pl.loop(0, width // COLS)
    def _(n):
        cols = pl.ds(pl.multiple_of(n * COLS, COLS), COLS)
        wide[:, cols] = dot_tn(o_ref[...], big[:, cols])
    wo_copy = pltpu.make_async_copy(wide, dwo_out, lsem.at[1])
    wo_copy.start()
    load_act = pltpu.make_async_copy(a_hbm, big, lsem.at[2])
    load_act.start()

    def finish_out(cols, total):
        out_ref[:, cols] = (x_ref[:, cols].astype(F32) + total).astype(BF16)
    out_rs.last(finish_out)

    kv_rs.near_second()
    own = rows_of(p.me * block, block)

    def finish_kv(cols, total):
        dkv_full[own, :head] = rope(total[:, :head], cos_ref[own, :], -sin_ref[own, :]).astype(BF16)
        dkv_full[own, head:] = total[:, head:].astype(BF16)
    kv_rs.last(finish_kv)
    kv_ag.start()
    da_rs.near_second()

    load_act.wait()
    slots = width // COLS

    def weight_grad(lhs, dst, drain):
        @pl.loop(0, slots)
        def _(n):
            if drain:
                pltpu.make_async_copy(tiles.at[n], dst.at[pl.ds(pl.multiple_of(n * COLS, COLS), COLS)], tsem.at[n]).wait()
            cols = pl.ds(pl.multiple_of(n * COLS, COLS), COLS)
            tiles[n] = dot_tn(lhs(), big[:, cols]).T
            pltpu.make_async_copy(tiles.at[n], dst.at[cols], tsem.at[n]).start()

    weight_grad(lambda: dq_ref[...], dwq_out, False)
    kv_ag.recv(0, 3)
    kv_ag.relay()
    kv_ag.forward(0, 3)
    kv_ag.recv(1, 2)
    kv_ag.forward(1, 2)
    kv_ag.recv(4, 5)
    kv_ag.forward(4, 5)
    kv_ag.recv(6, 7, 8, 9, 10, 11, 12)
    weight_grad(lambda: dkv_full[:, :head], dwk_out, True)
    weight_grad(lambda: dkv_full[:, head:], dwv_out, True)

    wo_copy.wait()

    def finish_da(cols, total):
        wide[:, cols] = (total + dot_nt(dkv_full[own, :head], wk_ref[cols, :])
                         + dot_nt(dkv_full[own, head:], wv_ref[cols, :]))
    da_rs.last(finish_da)

    dw_me[...] = jnp.zeros(dw_me.shape, F32)

    @pl.loop(0, block // 32)
    def _(n):
        rows = pl.ds(pl.multiple_of(n * 32, 32), 32)
        x_f = x_ref[rows, :].astype(F32)
        inv = lax.rsqrt(jnp.mean(x_f * x_f, axis=-1, keepdims=True) + 1e-6)
        normed = x_f * inv
        da = wide[rows, :]
        dw_me[...] += jnp.sum(da * normed, axis=0, keepdims=True)
        gn = da * gain_ref[...]
        dx_ref[rows, :] = (dout_ref[rows, :].astype(F32)
                           + inv * (gn - normed * jnp.mean(gn * normed, axis=-1, keepdims=True))).astype(BF16)

    lanes = 128
    for t in range(width // lanes):
        dw_all[0, t:t + 1, :] = dw_me[:, t * lanes:(t + 1) * lanes]
    for d in range(1, size):
        remote(dw_all.at[0], dw_all.at[d], ss_w.at[d], rs_w.at[d], peers[d - 1]).start()
    for d in range(1, size):
        remote(dw_all.at[d], dw_all.at[d], ss_w.at[d], rs_w.at[d], p.sib).wait_recv()
    dw_ref[...] = jnp.sum(dw_all[...], axis=0)

    for d in range(1, size):
        remote(dw_all.at[0], dw_all.at[0], ss_w.at[d], rs_w.at[d], p.sib).wait_send()
    kv_rs.chip_done()
    kv_rs.ring_done()
    da_rs.chip_done()
    da_rs.ring_done()
    kv_ag.finish()
    for n in range(slots):
        pltpu.make_async_copy(tiles.at[n], dwv_out.at[pl.ds(n * COLS, COLS)], tsem.at[n]).wait()


def local_block(size, hidden, positions, norm_w, w_query, w_key, w_value, w_out, grad_out):
    _, block, width = hidden.shape
    seq = positions.shape[1]
    head = w_key.shape[1]
    half = head // 2
    x, dout = hidden[0], grad_out[0]
    gain = (1.0 + norm_w)[None, :]
    inv_freq = 10000.0 ** (-2.0 * jnp.arange(half, dtype=F32) / head)
    angle = positions[0].astype(F32)[:, None] * inv_freq
    vm = pl.BlockSpec(memory_space=pltpu.VMEM)
    hbm = pl.BlockSpec(memory_space=pl.ANY)
    dma = pltpu.SemaphoreType.DMA
    shape = jax.ShapeDtypeStruct
    V = pltpu.VMEM

    a_full, dout_full, q, k, v, o, lse, cos_t, sin_t = pl.pallas_call(
        functools.partial(gather_kernel, size),
        out_shape=[shape((seq, width), BF16)] * 2 + [shape((seq, head), BF16)] * 4
        + [shape((seq, 128), F32), shape((seq, half), F32), shape((seq, half), F32)],
        in_specs=[vm] * 4 + [hbm] * 3,
        out_specs=[hbm] * 2 + [vm] * 7,
        scratch_shapes=[V((seq, width), BF16), V((3, width, head), BF16), V((seq // TILE, TILE, TILE), F32),
                        V((TILE, 128), F32), V((TILE, 128), F32), V((TILE, head), F32),
                        dma((5,)), dma((13,)), dma((13,)), dma((13,)), dma((13,))],
        compiler_params=pltpu.CompilerParams(collective_id=0, has_side_effects=True, vmem_limit_bytes=VMEM_LIMIT),
        name='gather_forward',
    )(x, dout, gain, angle, w_query, w_key, w_value)

    half_block = block // 2

    def ring_bufs(cols, dtype):
        return [V((4, block, cols), dtype), V((half_block, cols), dtype), V((half_block, cols), dtype),
                V((block, cols), dtype), V((block, cols), dtype)]
    kv_bufs = ring_bufs(2 * head, F32)
    out, dx, dwq, dwo, dwk, dwv, dw = pl.pallas_call(
        functools.partial(reduce_kernel, size),
        out_shape=[shape((block, width), BF16)] * 2
        + [shape((width, head), F32), shape((head, width), F32), shape((width, head), F32), shape((width, head), F32),
           shape((width // 128, 128), F32)],
        in_specs=[vm] * 14 + [hbm] * 2,
        out_specs=[vm] * 2 + [hbm] * 4 + [vm],
        scratch_shapes=[V((seq, width), BF16), V((seq, head), BF16), V((seq, 2 * head), F32), V((seq, 2 * head), BF16),
                        V((TILE, head), F32), V((2, block, width), BF16), V((3, block, width), BF16)]
        + ring_bufs(width, BF16) + ring_bufs(width, BF16)
        + [kv_bufs[0], V((3, block, 2 * head), F32)] + kv_bufs[1:]
        + [V((head, width), F32), V((width // COLS, COLS, head), F32), V((1, width), F32), V((size, width // 128, 128), F32),
           dma((3,)), dma((width // COLS,))] + [dma((10,))] * 6 + [dma((13,))] * 2 + [dma((size,))] * 2,
        compiler_params=pltpu.CompilerParams(collective_id=1, has_side_effects=True, vmem_limit_bytes=VMEM_LIMIT),
        name='reduce_backward',
    )(x, dout, gain, q, k, v, o, lse, cos_t, sin_t, w_out, w_query, w_key, w_value, a_full, dout_full)
    return out[None], dx[None], dwq, dwo, dwk, dwv, dw.reshape(width)


def solution(mesh):
    specs_in = (P('dp', 'tp', None), P('dp', None), P(None), P(None, 'tp'), P(None, None), P(None, None), P('tp', None), P('dp', 'tp', None))
    specs_out = (P('dp', 'tp', None), P('dp', 'tp', None), P('dp', 'tp'), P(('dp', 'tp'), None), P('dp', None), P('dp', None), P('dp'))
    return jax.shard_map(functools.partial(local_block, mesh.shape['tp']), mesh=mesh, in_specs=specs_in, out_specs=specs_out, check_vma=False)
```

time: 379 us -> 226 us (0.60); the launches traced: 375 us -> 226 us
  Pallas kernels: 0 us -> 209 us
  waiting for transfers between devices: 169 us -> 0 us
  matrix products: 121 us -> 0 us
  other arithmetic: 45.4 us -> 3.32 us
  between operations: 14.6 us -> 0.68 us
  blocking collectives: 13.9 us -> 0 us
    pallas_call x0 -> x2, Pallas kernels: none -> 209 us  [the longest x1 129 us: local_block(): pl.pallas_call(functools.partial(reduce_kernel, size), out_shape=[shape((...]
    dot_general x18 -> x0, matrix products: 121 us -> none  [the longest x1 15 us: local_block(): jnp.einsum('bse,de->bsd', grad_value, w_value, preferred_element_type=jnp...]
    all_gather x2 -> x0, waiting for transfers between devices: 65.9 us -> none  [the longest x1 49.5 us: local_block(): act_full = lax.all_gather(act_local, 'tp', axis=1, tiled=True)]
    psum x1 -> x0, waiting for transfers between devices: 63.4 us -> none  [local_block(): grad_w_key, grad_w_value = lax.psum((grad_w_key, grad_w_value), 'tp')]
    reduce_scatter x2 -> x0, waiting for transfers between devices: 39.1 us -> none  [the longest x1 35.4 us: local_block(): lax.psum_scatter(out_part, 'tp', scatter_dimension=1, tiled=True)]
    concatenate x4 -> x0, other arithmetic: 17.6 us -> none  [apply_rope(): jnp.concatenate([first * cos_t - second * sin_t, second * cos_t + first *...]
    psum x1 -> x0, blocking collectives: 13.9 us -> none  [local_block(): grad_norm_w = lax.psum(grad_norm_part, 'tp')]
    reduce_sum x3 -> x0, other arithmetic: 11 us -> none  [the longest x1 7.33 us: local_block(): attn_probs = jax.nn.softmax(jnp.where(causal, scores, -1e+30), axis=-1)]
  transfers between devices with their start and end apart: 5 -> 0, of which waited for: 5 -> 0; matrix products, arithmetic and copies ran while one was open for 22% -> 0% of each run, Pallas kernels for 0% -> 0%
where the time goes in v1:
time: 226 us
  Pallas kernels  209 us (92%)
  local copies, waits for them, and re-layouts  12.4 us (5%)
  other arithmetic  3.32 us (1%)
    pallas_call x1, Pallas kernels, local_block(): pl.pallas_call(functools.partial(reduce_kernel, size), out_shape=[shape((...  129 us
    pallas_call x1, Pallas kernels, local_block(): pl.pallas_call(functools.partial(gather_kernel, size), out_shape=[shape((...  81 us
    unnamed x19, local copies, waits for them, and re-layouts  12.4 us

profile of v1, /device:TPU:81, one launch (start us, length us, event | category | flops | bytes accessed | tf_op | source)
XLA Modules:
  0.0 225.9 jit_solution(5197297750259567397)
XLA Ops:
  0.6 0.7 convert_element_type.10
  1.4 1.3 broadcast_add_fusion
  2.6 1.3 broadcast_multiply_fusion.angle_ref
  4.0 81.0 %gather_forward.1 = (bf16[2048,2048]{1,0:T(8,128)(2,1)}, bf16[2048,2048]{1,0:T(8,128)(2,1)}, bf16[2048,256]{1,0:T(8,128)(2,1)}, bf16[2048,256]{1,0:T(8,128)(2,1)...) custom-call(bf16[256,2048]{1,0:T(8,128)(2,1)} %bitcast.7, ...), custom_call_target="tpu_custom_call" | custom-call | tf_op jit(solution)/shard_map/gather_forward/pallas_call | solution.py:501
  84.9 128.5 %reduce_backward.1 = (bf16[256,2048]{1,0:T(8,128)(2,1)}, bf16[256,2048]{1,0:T(8,128)(2,1)}, f32[2048,256]{1,0:T(8,128)}, f32[256,2048]{1,0:T(8,128)}, f32[2048,2...) custom-call(bf16[256,2048]{1,0:T(8,128)(2,1)} %bitcast.8, bf16[256,2048]{1,0:T(8,128)(2,1)} %bitcast.10, ...), custom_call_target="tpu_custom_call" | custom-call | tf_op jit(solution)/shard_map/reduce_backward/pallas_call | solution.py:520
  213.5 0.0 copy-start.4
  213.5 0.0 copy-start.3
  213.5 2.5 %copy.22 = bf16[1,256,2048]{2,1,0:T(8,128)(2,1)} copy(bf16[1,256,2048]{2,1,0:T(8,128)(2,1)} %bitcast.12) | data formatting | bytes 2097152
  215.9 0.0 copy-done.4
  215.9 1.0 copy.23
  216.9 0.0 copy-done.3
  216.9 0.0 copy-start.2
  216.9 1.3 copy.24
  218.2 1.0 copy-done.2
  219.3 0.0 copy-start.1
  219.3 1.3 copy.25
  220.6 1.0 copy-done.1
  221.6 0.0 copy-start
  221.6 1.3 copy.26
  222.9 1.0 copy-done
  224.0 0.0 copy-start.5
  224.0 1.3 copy.27
  225.3 0.0 copy-done.5
  225.3 0.6 copy.28
  (1 shorter events, 0.0 us)
Async XLA Ops:
  213.5 2.5 %copy-start.4 = (bf16[256,2048]{1,0:T(8,128)(2,1)S(1)}, bf16[256,2048]{1,0:T(8,128)(2,1)}, u32[]{:S(2)}) copy-start(bf16[256,2048]{1,0:T(8,128)(2,1)} %get-tuple-element.33) | copy-start | bytes 3145732
  213.5 3.4 %copy-start.3 = (f32[2048,256]{1,0:T(8,128)S(1)}, f32[2048,256]{1,0:T(8,128)}, u32[]{:S(2)}) copy-start(f32[2048,256]{1,0:T(8,128)} %get-tuple-element.48) | copy-start | bytes 6291460
  216.9 2.3 %copy-start.2 = (f32[256,2048]{1,0:T(8,128)S(1)}, f32[256,2048]{1,0:T(8,128)}, u32[]{:S(2)}) copy-start(f32[256,2048]{1,0:T(8,128)} %get-tuple-element.49) | copy-start | bytes 6291460
  219.3 2.3 %copy-start.1 = (f32[2048,256]{1,0:T(8,128)S(1)}, f32[2048,256]{1,0:T(8,128)}, u32[]{:S(2)}) copy-start(f32[2048,256]{1,0:T(8,128)} %get-tuple-element.50) | copy-start | bytes 6291460
  221.6 2.3 %copy-start = (f32[2048,256]{1,0:T(8,128)S(1)}, f32[2048,256]{1,0:T(8,128)}, u32[]{:S(2)}) copy-start(f32[2048,256]{1,0:T(8,128)} %get-tuple-element.51) | copy-start | bytes 6291460
  224.0 1.3 copy-start.5

commit v2 on v0

v2 whole, which is shorter than its diff:
```python
import functools

import jax
import jax.numpy as jnp
from jax import lax
from jax.experimental import pallas as pl
from jax.experimental.pallas import tpu as pltpu
from jax.sharding import PartitionSpec as P

MESH = pl.DeviceIdType.MESH
F32 = jnp.float32
BF16 = jnp.bfloat16
TILE = 512
COLS = 512
VMEM_LIMIT = 63 * 1024 * 1024


def dot_nn(a, b):
    return lax.dot_general(a, b, (((1,), (0,)), ((), ())), preferred_element_type=F32)


def dot_nt(a, b):
    return lax.dot_general(a, b, (((1,), (1,)), ((), ())), preferred_element_type=F32)


def dot_tn(a, b):
    return lax.dot_general(a, b, (((0,), (0,)), ((), ())), preferred_element_type=F32)


def rope(u, cos_t, sin_t):
    half = u.shape[-1] // 2
    first, second = u[:, :half], u[:, half:]
    return jnp.concatenate([first * cos_t - second * sin_t, second * cos_t + first * sin_t], axis=-1)


class Place:
    def __init__(self, size, stride):
        n = size // 2
        group = lax.axis_index('dp')
        z, y = lax.rem(group, 2), lax.rem(lax.div(group, stride), 2)
        self.group_z = group + 1 - 2 * z
        self.group_y = group + stride * (1 - 2 * y)
        self.part = 2 * y + z
        self.part_z, self.part_y, self.part_d = 2 * y + 1 - z, 2 * (1 - y) + z, 3 - self.part
        self.me = lax.axis_index('tp')
        self.core = lax.rem(self.me, 2)
        self.chip = lax.div(self.me, 2)
        self.chip_r = lax.rem(self.chip + 1, n)
        self.chip_l = lax.rem(self.chip + n - 1, n)
        self.chip_o = lax.rem(self.chip + 2, n)
        self.right = self.chip_r * 2 + self.core
        self.left = self.chip_l * 2 + self.core
        self.sib = self.chip * 2 + 1 - self.core


def remote(src, dst, ssem, rsem, to):
    return pltpu.make_async_remote_copy(src_ref=src, dst_ref=dst, send_sem=ssem, recv_sem=rsem,
                                        device_id={'tp': to}, device_id_type=MESH)


def rows_of(start, size):
    return pl.ds(pl.multiple_of(start, min(size, 128)), size)


class Gather:
    def __init__(self, place, at, ssem, rsem):
        self.at, self.p, self.ssem, self.rsem = at, place, ssem, rsem
        p = place
        self.own = [at(p.chip, p.core, h) for h in (0, 1)]
        self.own_all = at(p.chip, p.core, None)
        regions = []
        for core in (p.core, 1 - p.core):
            for chip in (p.chip_l, p.chip_r, p.chip_o):
                regions += [at(chip, core, 0), at(chip, core, 1)]
        self.regions = regions[:6] + [at(p.chip, 1 - p.core, None)] + regions[6:]

    def _send(self, sem, src, dst, rsem, to):
        remote(src, dst, self.ssem.at[sem], self.rsem.at[rsem], to).start()

    def start(self, parts=None, whole=None):
        p = self.p
        parts = self.own if parts is None else parts
        whole = self.own_all if whole is None else whole
        self._send(0, parts[0], self.own[0], 0, p.right)
        self._send(3, parts[1], self.own[1], 3, p.left)
        self._send(1, parts[1], self.own[1], 1, p.right)
        self._send(2, parts[0], self.own[0], 2, p.left)
        self._send(6, whole, self.own_all, 6, p.sib)

    def recv(self, *which):
        for k in which:
            ref = self.regions[k]
            remote(ref, ref, self.ssem.at[k], self.rsem.at[k], self.p.sib).wait_recv()

    def _forward_only(self, *which):
        for k in which:
            self._send(7 + k, self.regions[k], self.regions[k], 7 + k, self.p.sib)

    def _forward(self, *which):
        self.recv(*which)
        self._forward_only(*which)

    def first(self):
        self.recv(0, 3)
        self._send(4, self.regions[0], self.regions[0], 4, self.p.right)
        self._send(5, self.regions[3], self.regions[3], 5, self.p.left)
        self._forward_only(0, 3)

    def second(self):
        self._forward(1, 2)

    def third(self):
        self._forward(4, 5)

    def sibling(self):
        self.recv(6)

    def sibling_near(self):
        self.recv(7, 8, 9, 10)

    def sibling_far(self):
        self.recv(11, 12)

    def finish(self):
        for k in range(13):
            ref = self.own_all if k == 6 else self.own[0]
            remote(ref, ref, self.ssem.at[k], self.rsem.at[k], self.p.sib).wait_send()


class Share:
    def __init__(self, place, full, rows, ssem, rsem):
        self.p, self.full, self.rows, self.ssem, self.rsem = place, full, rows, ssem, rsem

    def at(self, part, h=None, other=False):
        core = 1 - self.p.core if other else self.p.core
        if h is None:
            return self.full.at[:, core, part]
        return self.full.at[:, core, part, pl.ds(h * self.rows, self.rows)]

    def _send(self, k, ref, **to):
        pltpu.make_async_remote_copy(src_ref=ref, dst_ref=ref, send_sem=self.ssem.at[k], recv_sem=self.rsem.at[k],
                                     device_id=to, device_id_type=MESH).start()

    def _recv(self, k, ref):
        remote(ref, ref, self.ssem.at[k], self.rsem.at[k], self.p.sib).wait_recv()

    def start(self):
        p = self.p
        self._send(0, self.at(p.part), dp=p.group_z)
        self._send(1, self.at(p.part), dp=p.group_y)

    def relay(self):
        p = self.p
        self._recv(0, self.at(p.part_z))
        self._send(2, self.at(p.part_z, 0), dp=p.group_y)
        self._recv(1, self.at(p.part_y))
        self._send(3, self.at(p.part_y, 1), dp=p.group_z)
        self._send(4, self.at(p.part_z), tp=p.sib)
        self._send(5, self.at(p.part_y), tp=p.sib)

    def forward(self):
        p = self.p
        for h in (0, 1):
            self._recv(2 + h, self.at(p.part_d, h))
            self._send(6 + h, self.at(p.part_d, h), tp=p.sib)

    def finish(self):
        p = self.p
        for k, h in enumerate((None, None, 0, 0, None, None, 0, 0)):
            ref = self.at(p.part, h)
            remote(ref, ref, self.ssem.at[k], self.rsem.at[k], p.sib).wait_send()
        self._recv(4, self.at(p.part_z, None, True))
        self._recv(5, self.at(p.part_y, None, True))
        self._recv(6, self.at(p.part_d, 0, True))
        self._recv(7, self.at(p.part_d, 1, True))


class Exchange:
    def __init__(self, place, block, src, dst, relays, ssem, rsem):
        self.p, self.block, self.src, self.dst, self.relays, self.ssem, self.rsem = place, block, src, dst, relays, ssem, rsem

    def _send(self, sem, src, dst, rsem, to):
        remote(src, dst, self.ssem.at[sem], self.rsem.at[rsem], to).start()

    def part(self, chip, core):
        return self.src.at[rows_of((chip * 2 + core) * self.block, self.block)]

    def start(self):
        p = self.p
        slot = self.dst.at[p.me]
        self._send(0, self.part(p.chip_o, 0), self.relays.at[0], 0, p.right)
        self._send(1, self.part(p.chip_o, 1), self.relays.at[1], 1, p.left)
        for core in (0, 1):
            self._send(2 + core, self.part(p.chip_r, core), slot, 2 + p.core, p.chip_r * 2 + core)
            self._send(4 + core, self.part(p.chip_l, core), slot, 4 + p.core, p.chip_l * 2 + core)
        self._send(8, self.part(p.chip, 1 - p.core), slot, 8, p.sib)
        self.dst[p.me] = self.src[rows_of(p.me * self.block, self.block), :]

    def _recv(self, k, ref):
        remote(ref, ref, self.ssem.at[k], self.rsem.at[k], self.p.sib).wait_recv()

    def relay(self):
        p = self.p
        self._recv(0, self.relays.at[0])
        self._send(6, self.relays.at[0], self.dst.at[p.left], 6 + p.core, p.chip_r * 2)
        self._recv(1, self.relays.at[1])
        self._send(7, self.relays.at[1], self.dst.at[p.right], 6 + p.core, p.chip_l * 2 + 1)

    def recv(self):
        p = self.p
        for core in (0, 1):
            self._recv(2 + core, self.dst.at[p.chip_l * 2 + core])
            self._recv(4 + core, self.dst.at[p.chip_r * 2 + core])
            self._recv(6 + core, self.dst.at[p.chip_o * 2 + core])
        self._recv(8, self.dst.at[p.sib])

    def finish(self):
        for k in range(9):
            ref = self.relays.at[0]
            remote(ref, ref, self.ssem.at[k], self.rsem.at[k], self.p.sib).wait_send()


class Scatter:
    def __init__(self, place, block, src, d2d, sums, top, bot, from_l, from_r, ssem, rsem):
        self.__dict__.update(locals())
        self.half = block // 2

    def rows(self, chip, core, h=None):
        row = (chip * 2 + core) * self.block
        return rows_of(row, self.block) if h is None else rows_of(row + h * self.half, self.half)

    def _send(self, k, src, dst, to):
        remote(src, dst, self.ssem.at[k], self.rsem.at[k], to).start()

    def _recv(self, k, ref):
        remote(ref, ref, self.ssem.at[k], self.rsem.at[k], self.place.sib).wait_recv()

    def chip_send(self):
        p = self.place
        for k, chip in enumerate((p.chip_o, p.chip_r, p.chip_l, p.chip)):
            self._send(k, self.src.at[self.rows(chip, 1 - p.core)], self.d2d.at[k], p.sib)

    def far(self):
        p, half = self.place, self.half
        self._recv(0, self.d2d.at[0])
        self.sums[0] = self.src[self.rows(p.chip_o, p.core), :] + self.d2d[0]
        self._send(4, self.sums.at[0, pl.ds(0, half)], self.top, p.right)
        self._send(5, self.sums.at[0, pl.ds(half, half)], self.bot, p.left)

    def near_half(self, k, h, chip, extra, dst, sem, to):
        rows = pl.ds(h * self.half, self.half)
        total = self.src[self.rows(chip, self.place.core, h), :] + self.d2d[k, rows, :]
        self.sums[k, rows, :] = total if extra is None else total + extra[...]
        self._send(sem, self.sums.at[k, rows], dst.at[rows], to)

    def near_first(self):
        p = self.place
        self._recv(1, self.d2d.at[1])
        self.near_half(1, 1, p.chip_r, None, self.from_l, 6, p.right)
        self._recv(2, self.d2d.at[2])
        self.near_half(2, 0, p.chip_l, None, self.from_r, 8, p.left)

    def near_second(self):
        p = self.place
        self._recv(4, self.top)
        self.near_half(1, 0, p.chip_r, self.top, self.from_l, 7, p.right)
        self._recv(5, self.bot)
        self.near_half(2, 1, p.chip_l, self.bot, self.from_r, 9, p.left)

    def last(self):
        p, half = self.place, self.half
        self._recv(3, self.d2d.at[3])
        for k, ref, h in ((6, self.from_l, 1), (7, self.from_l, 0), (8, self.from_r, 0), (9, self.from_r, 1)):
            self._recv(k, ref.at[pl.ds(h * half, half)])
        return self.src[self.rows(p.chip, p.core), :] + self.d2d[3] + self.from_l[...] + self.from_r[...]

    def finish(self):
        for k in range(10):
            ref = self.d2d.at[0] if k < 4 else self.top
            remote(ref, ref, self.ssem.at[k], self.rsem.at[k], self.place.sib).wait_send()


def block_kernel(size, stride, x_ref, dout_ref, gain_ref, angle_ref, wq_hbm, wk_hbm, wv_hbm, wo_hbm,
                 out_ref, dx_ref, dwo_out, dw_ref, a_out, dq_out, dkv_out, wo_full, wq_full,
                 act_full, big, wbuf, wo, wqt, q_ref, k_ref, v_ref, o_ref, dq_ref, dkv_ref, dkv_full, o_all, dq_all,
                 relay_o, relay_q, lse_ref, cos_ref, sin_ref, m_scr, l_scr, acc,
                 d2d, sums, top, bot, from_l, from_r, wide, dw_me, dw_all, lsem,
                 ss_a, rs_a, ss_d, rs_d, ss_wo, rs_wo, ss_wq, rs_wq, ss_kv, rs_kv, ss_yo, rs_yo, ss_yq, rs_yq,
                 ss_o, rs_o, ss_q, rs_q, ss_r, rs_r, ss_w, rs_w):
    p = Place(size, stride)
    block, width = x_ref.shape
    seq, head = q_ref.shape
    chips = size // 2
    half = block // 2
    parts, part_rows = wo.shape[:2]
    scale = head ** -0.5
    wo_rows = lambda: wo[...].reshape(head, width)

    barrier = pltpu.get_barrier_semaphore()
    peers = [lax.rem(p.me + d, size) for d in range(1, size)]
    for to in [{'tp': peer} for peer in peers] + [{'dp': p.group_z}, {'dp': p.group_y}]:
        pl.semaphore_signal(barrier, inc=1, device_id=to, device_id_type=MESH)

    loads = [pltpu.make_async_copy(src, dst, lsem.at[i]) for i, (src, dst) in enumerate(
        ((wq_hbm, wbuf.at[0]), (wo_hbm, wo), (wk_hbm, wbuf.at[1]), (wv_hbm, wbuf.at[2])))]
    for copy in loads:
        copy.start()

    def weight_at(full):
        quarter = part_rows // 2

        def at(chip, core, h):
            if h is None:
                return full.at[chip, core, p.part]
            return full.at[chip, core, p.part, pl.ds(h * quarter, quarter)]
        return at

    def rows_at(full):
        def at(chip, core, h):
            row = (chip * 2 + core) * block
            return full.at[rows_of(row, block) if h is None else rows_of(row + h * half, half)]
        return at

    def grad_at(chip, core, h):
        return big.at[chip, core] if h is None else big.at[chip, core, pl.ds(h * (parts // 2), parts // 2)]

    act = Gather(p, rows_at(act_full), ss_a, rs_a)
    grad = Gather(p, grad_at, ss_d, rs_d)
    wo_g = Gather(p, weight_at(wo_full), ss_wo, rs_wo)
    wq_g = Gather(p, weight_at(wq_full), ss_wq, rs_wq)
    kv_g = Gather(p, rows_at(dkv_full), ss_kv, rs_kv)
    wo_s = Share(p, wo_full, part_rows // 2, ss_yo, rs_yo)
    wq_s = Share(p, wq_full, part_rows // 2, ss_yq, rs_yq)
    o_x = Exchange(p, block, o_ref, o_all, relay_o, ss_o, rs_o)
    dq_x = Exchange(p, block, dq_ref, dq_all, relay_q, ss_q, rs_q)
    kv_r = Scatter(p, block, dkv_ref, d2d, sums, top, bot, from_l, from_r, ss_r, rs_r)

    def start_weight(g, shard, sem):
        quarter = part_rows // 2
        own = pltpu.make_async_copy(shard.at[p.part], g.own_all, lsem.at[sem])
        own.start()
        g.start([shard.at[p.part, pl.ds(h * quarter, quarter)] for h in (0, 1)], shard.at[p.part])
        return own

    loads[1].wait()
    loads[0].wait()
    pl.semaphore_wait(barrier, size + 1)
    own_wo = start_weight(wo_g, wo, 4)

    @pl.loop(0, parts)
    def _(n):
        rows = pl.ds(pl.multiple_of(n * COLS, COLS), COLS)
        flipped = wbuf[0, rows, :].T
        for g in range(parts):
            wqt[g, :, rows] = flipped[g * part_rows:(g + 1) * part_rows, :]
    own_wq = start_weight(wq_g, wqt, 5)

    @pl.loop(0, block // 64)
    def _(n):
        rows = pl.ds(pl.multiple_of(n * 64, 64), 64)
        x_f = x_ref[rows, :].astype(F32)
        inv = lax.rsqrt(jnp.mean(x_f * x_f, axis=-1, keepdims=True) + 1e-6)
        act_full[rows_of(p.me * block + n * 64, 64), :] = (x_f * inv * gain_ref[...]).astype(BF16)

    for g in (wo_g, wq_g):
        g.first()
    act.start()

    @pl.loop(0, seq // 64)
    def _(n):
        rows = pl.ds(pl.multiple_of(n * 64, 64), 64)
        angle = angle_ref[rows, :]
        cos_ref[rows, :] = jnp.cos(angle)
        sin_ref[rows, :] = jnp.sin(angle)

    loads[2].wait()
    loads[3].wait()

    def project(first, second):
        @pl.loop(0, 2)
        def _(n):
            rows = rows_of((first + n * (second - first)) * block, block)
            a = act_full[rows, :]
            cos_t, sin_t = cos_ref[rows, :], sin_ref[rows, :]
            query = dot_nn(a, wbuf[0]).astype(BF16).astype(F32)
            q_ref[rows, :] = (rope(query, cos_t, sin_t) * scale).astype(BF16)
            key = dot_nn(a, wbuf[1]).astype(BF16).astype(F32)
            k_ref[rows, :] = rope(key, cos_t, sin_t).astype(BF16)
            v_ref[rows, :] = dot_nn(a, wbuf[2]).astype(BF16)

    for g, s, own in ((wo_g, wo_s, own_wo), (wq_g, wq_s, own_wq)):
        g.second()
        g.third()
        own.wait()
        s.start()

    act.sibling()
    project(p.me, p.sib)
    act.first()
    grad.start([dout_ref.at[pl.ds(h * (parts // 2), parts // 2)] for h in (0, 1)], dout_ref)
    big[p.chip, p.core] = dout_ref[...]
    act.second()
    project(p.left, p.right)
    act.sibling_near()
    project(p.chip_l * 2 + 1 - p.core, p.chip_r * 2 + 1 - p.core)
    act.third()
    act.sibling_far()
    project(p.chip_o * 2 + p.core, p.chip_o * 2 + 1 - p.core)
    a_copy = pltpu.make_async_copy(act_full, a_out, lsem.at[6])
    a_copy.start()

    row_ids = lax.broadcasted_iota(jnp.int32, (TILE, TILE), 0)
    col_ids = lax.broadcasted_iota(jnp.int32, (TILE, TILE), 1)

    def tile_rows(j):
        return pl.ds(pl.multiple_of(j * TILE, TILE), TILE)

    @pl.loop(0, seq // TILE)
    def _(i):
        rows = tile_rows(i)
        m_scr[...] = jnp.full(m_scr.shape, -1e30, F32)
        l_scr[...] = jnp.zeros(l_scr.shape, F32)
        acc[...] = jnp.zeros(acc.shape, F32)

        @pl.loop(0, i + 1)
        def _(j):
            s = dot_nt(q_ref[rows, :], k_ref[tile_rows(j), :])
            s = jnp.where(row_ids + (i - j) * TILE >= col_ids, s, -1e30)
            dkv_ref[tile_rows(j), :] = s
            m_old = m_scr[:, :1]
            m_new = jnp.maximum(m_old, jnp.max(s, axis=-1, keepdims=True))
            l_new = l_scr[:, :1] * jnp.exp(m_old - m_new) + jnp.sum(jnp.exp(s - m_new), axis=-1, keepdims=True)
            m_scr[...] = jnp.broadcast_to(m_new, m_scr.shape)
            l_scr[...] = jnp.broadcast_to(l_new, l_scr.shape)

        lse_ref[rows, :] = m_scr[...] + jnp.log(l_scr[...])

        @pl.loop(0, i + 1)
        def _(j):
            prob = jnp.exp(dkv_ref[tile_rows(j), :] - lse_ref[rows, :1]).astype(BF16)
            acc[...] += dot_nn(prob, v_ref[tile_rows(j), :])

        o_ref[rows, :] = acc[...].astype(BF16)

    dkv_ref[...] = jnp.zeros(dkv_ref.shape, F32)

    def backward(first, second, count):
        @pl.loop(0, count)
        def _(n):
            i = first + n * (second - first)
            rows = tile_rows(i)
            do = dot_nt(big[i].reshape(TILE, width), wo_rows()).astype(BF16)
            row_dot = jnp.sum(do.astype(F32) * o_ref[rows, :].astype(F32), axis=-1, keepdims=True)
            acc[...] = jnp.zeros(acc.shape, F32)
            q = q_ref[rows, :]

            @pl.loop(0, i + 1)
            def _(j):
                cols = tile_rows(j)
                s = dot_nt(q, k_ref[cols, :])
                prob = jnp.exp(s - lse_ref[rows, :1])
                prob = jnp.where(row_ids + (i - j) * TILE >= col_ids, prob, 0.0)
                dkv_ref[cols, head:] += dot_tn(prob.astype(BF16), do)
                dprob = dot_nt(do, v_ref[cols, :])
                ds = (prob * (dprob - row_dot)).astype(BF16)
                dkv_ref[cols, :head] += dot_tn(ds, q)
                acc[...] += dot_nn(ds, k_ref[cols, :])

            dq_ref[rows, :] = rope(acc[...] * scale, cos_ref[rows, :], -sin_ref[rows, :]).astype(BF16)

    grad.sibling()
    backward(p.chip, p.chip, 1)
    grad.first()
    o_x.start()
    for s in (wo_s, wq_s):
        s.relay()
    grad.second()
    grad.sibling_near()
    backward(p.chip_l, p.chip_r, 2)
    grad.third()
    grad.sibling_far()
    backward(p.chip_o, p.chip_o, 1)
    dq_copy = pltpu.make_async_copy(dq_ref, dq_out, lsem.at[7])
    dq_copy.start()

    kv_r.chip_send()
    o_x.relay()
    kv_r.far()
    kv_r.near_first()
    dq_x.start()
    for s in (wo_s, wq_s):
        s.forward()

    def col_tiles(fn):
        @pl.loop(0, width // COLS)
        def _(n):
            fn(pl.ds(pl.multiple_of(n * COLS, COLS), COLS))

    def big_cols(cols):
        return big[:, :, :, :, cols].reshape(seq, COLS)

    def weight_o(cols):
        wide[:, cols] = dot_tn(o_ref[...], big_cols(cols))
    col_tiles(weight_o)
    wo_copy = pltpu.make_async_copy(wide, dwo_out, lsem.at[1])
    wo_copy.start()

    kv_r.near_second()
    grad.finish()
    wo_g.sibling()
    wo_g.sibling_near()
    wo_g.sibling_far()
    wo_s.finish()
    load_wo = pltpu.make_async_copy(wo_full, big, lsem.at[2])
    load_wo.start()
    dq_x.relay()
    o_x.recv()
    load_wo.wait()

    def finish_out(cols):
        total = dot_nn(jnp.concatenate([o_all[h] for h in range(size)], axis=-1), big_cols(cols))
        out_ref[:, cols] = (x_ref[:, cols].astype(F32) + total).astype(BF16)
    col_tiles(finish_out)

    wq_g.sibling()
    wq_g.sibling_near()
    wq_g.sibling_far()
    wq_s.finish()
    load_wq = pltpu.make_async_copy(wq_full, big, lsem.at[3])
    load_wq.start()

    own = rows_of(p.me * block, block)
    total = kv_r.last()
    dkv_full[own, :head] = rope(total[:, :head], cos_ref[own, :], -sin_ref[own, :]).astype(BF16)
    dkv_full[own, head:] = total[:, head:].astype(BF16)
    kv_g.start()
    dq_x.recv()
    wo_copy.wait()
    load_wq.wait()

    def finish_da(cols):
        total = dot_nn(jnp.concatenate([dq_all[h] for h in range(size)], axis=-1), big_cols(cols))
        wide[:, cols] = (total + dot_nt(dkv_full[own, :head], wbuf[1, cols, :])
                         + dot_nt(dkv_full[own, head:], wbuf[2, cols, :]))
    col_tiles(finish_da)
    kv_g.first()

    dw_me[...] = jnp.zeros(dw_me.shape, F32)
    sub = 32

    @pl.loop(0, block // sub)
    def _(n):
        rows = pl.ds(pl.multiple_of(n * sub, sub), sub)
        x_f = x_ref[rows, :].astype(F32)
        inv = lax.rsqrt(jnp.mean(x_f * x_f, axis=-1, keepdims=True) + 1e-6)
        normed = x_f * inv
        da = wide[rows, :]
        dw_me[...] += jnp.sum(da * normed, axis=0, keepdims=True)
        gn = da * gain_ref[...]
        per = part_rows // sub
        dout = dout_ref[n // per, pl.ds(pl.multiple_of(lax.rem(n, per) * sub, sub), sub), :].astype(F32)
        dx_ref[rows, :] = (dout + inv * (gn - normed * jnp.mean(gn * normed, axis=-1, keepdims=True))).astype(BF16)

    lanes = 128
    for t in range(width // lanes):
        dw_all[0, t:t + 1, :] = dw_me[:, t * lanes:(t + 1) * lanes]
    for d in range(1, size):
        remote(dw_all.at[0], dw_all.at[d], ss_w.at[d], rs_w.at[d], peers[d - 1]).start()
    kv_g.second()
    kv_g.third()
    for d in range(1, size):
        remote(dw_all.at[d], dw_all.at[d], ss_w.at[d], rs_w.at[d], p.sib).wait_recv()
    dw_ref[...] = jnp.sum(dw_all[...], axis=0)
    kv_g.sibling()
    kv_g.sibling_near()
    kv_g.sibling_far()
    kv_copy = pltpu.make_async_copy(dkv_full, dkv_out, lsem.at[2])
    kv_copy.start()

    for d in range(1, size):
        remote(dw_all.at[0], dw_all.at[0], ss_w.at[d], rs_w.at[d], p.sib).wait_send()
    for g in (act, wo_g, wq_g, kv_g, kv_r, o_x, dq_x):
        g.finish()
    a_copy.wait()
    dq_copy.wait()
    kv_copy.wait()


def weight_kernel(a_ref, dq_ref, dkv_ref, dwq_ref, dwk_ref, dwv_ref):
    head = dq_ref.shape[1]
    a = a_ref[...]
    dwq_ref[...] = dot_tn(dq_ref[...], a).T
    dwk_ref[...] = dot_tn(dkv_ref[:, :head], a).T
    dwv_ref[...] = dot_tn(dkv_ref[:, head:], a).T


def local_block(size, stride, hidden, positions, norm_w, w_query, w_key, w_value, w_out, grad_out):
    _, block, width = hidden.shape
    seq = positions.shape[1]
    head = w_key.shape[1]
    half = head // 2
    chips, parts = size // 2, 4
    part_rows = block // parts
    x, dout = hidden[0], grad_out[0].reshape(parts, part_rows, width)
    gain = (1.0 + norm_w)[None, :]
    inv_freq = 10000.0 ** (-2.0 * jnp.arange(half, dtype=F32) / head)
    angle = positions[0].astype(F32)[:, None] * inv_freq
    vm = pl.BlockSpec(memory_space=pltpu.VMEM)
    hbm = pl.BlockSpec(memory_space=pl.ANY)
    dma = pltpu.SemaphoreType.DMA
    shape = jax.ShapeDtypeStruct
    V = pltpu.VMEM
    full = (chips, 2, parts, part_rows, width)
    kv = 2 * head

    out, dx, dwo, dw, act, dq, dkv, _, _ = pl.pallas_call(
        functools.partial(block_kernel, size, stride),
        out_shape=[shape((block, width), BF16)] * 2 + [shape((head, width), F32), shape((width // 128, 128), F32),
                                                       shape((seq, width), BF16), shape((seq, head), BF16),
                                                       shape((seq, kv), BF16), shape(full, BF16), shape(full, BF16)],
        in_specs=[vm] * 4 + [hbm] * 4,
        out_specs=[vm, vm, hbm, vm] + [hbm] * 5,
        scratch_shapes=[V((seq, width), BF16), V(full, BF16), V((3, width, head), BF16), V((parts, part_rows, width), BF16),
                        V((parts, part_rows, width), BF16)] + [V((seq, head), BF16)] * 5
        + [V((seq, kv), F32), V((seq, kv), BF16), V((size, block, head), BF16), V((size, block, head), BF16),
           V((2, block, head), BF16), V((2, block, head), BF16), V((seq, 128), F32), V((seq, half), F32), V((seq, half), F32),
           V((TILE, 128), F32), V((TILE, 128), F32), V((TILE, head), F32),
           V((4, block, kv), F32), V((3, block, kv), F32), V((block // 2, kv), F32), V((block // 2, kv), F32),
           V((block, kv), F32), V((block, kv), F32), V((head, width), F32), V((1, width), F32),
           V((size, width // 128, 128), F32), dma((8,))]
        + [dma((13,))] * 10 + [dma((8,))] * 4 + [dma((9,))] * 4 + [dma((10,))] * 2 + [dma((size,))] * 2,
        compiler_params=pltpu.CompilerParams(collective_id=0, has_side_effects=True, vmem_limit_bytes=VMEM_LIMIT),
        name='attention_block',
    )(x, dout, gain, angle, w_query, w_key, w_value, w_out.reshape(parts, part_rows, width))

    dwq, dwk, dwv = pl.pallas_call(
        weight_kernel,
        grid=(width // COLS,),
        out_shape=[shape((width, head), F32)] * 3,
        in_specs=[pl.BlockSpec((seq, COLS), lambda n: (0, n)), pl.BlockSpec((seq, head), lambda n: (0, 0)),
                  pl.BlockSpec((seq, kv), lambda n: (0, 0))],
        out_specs=[pl.BlockSpec((COLS, head), lambda n: (n, 0))] * 3,
        name='weight_grads',
    )(act, dq, dkv)
    return out[None], dx[None], dwq, dwo, dwk, dwv, dw.reshape(width)


def solution(mesh):
    specs_in = (P('dp', 'tp', None), P('dp', None), P(None), P(None, 'tp'), P(None, None), P(None, None), P('tp', None), P('dp', 'tp', None))
    specs_out = (P('dp', 'tp', None), P('dp', 'tp', None), P('dp', 'tp'), P(('dp', 'tp'), None), P('dp', None), P('dp', None), P('dp'))
    column = [tuple(d.coords) for d in mesh.devices[:, 0]]
    stride = sum(c[1] == column[0][1] for c in column)
    local = functools.partial(local_block, mesh.shape['tp'], stride)
    return jax.shard_map(local, mesh=mesh, in_specs=specs_in, out_specs=specs_out, check_vma=False)
```

time: 379 us -> 181 us (0.48); the launches traced: 375 us -> 181 us
  Pallas kernels: 0 us -> 173 us
  waiting for transfers between devices: 169 us -> 0 us
  matrix products: 121 us -> 0 us
  other arithmetic: 45.4 us -> 3.32 us
  between operations: 14.6 us -> 0.67 us
  blocking collectives: 13.9 us -> 0 us
  local copies, waits for them, and re-layouts: 10.1 us -> 4.49 us
    pallas_call x0 -> x2, Pallas kernels: none -> 173 us  [the longest x1 161 us: local_block(): pl.pallas_call(functools.partial(block_kernel, size, stride), out_shape=[...]
    dot_general x18 -> x0, matrix products: 121 us -> none  [the longest x1 15 us: local_block(): jnp.einsum('bse,de->bsd', grad_value, w_value, preferred_element_type=jnp...]
    all_gather x2 -> x0, waiting for transfers between devices: 65.9 us -> none  [the longest x1 49.5 us: local_block(): act_full = lax.all_gather(act_local, 'tp', axis=1, tiled=True)]
    psum x1 -> x0, waiting for transfers between devices: 63.4 us -> none  [local_block(): grad_w_key, grad_w_value = lax.psum((grad_w_key, grad_w_value), 'tp')]
    reduce_scatter x2 -> x0, waiting for transfers between devices: 39.1 us -> none  [the longest x1 35.4 us: local_block(): lax.psum_scatter(out_part, 'tp', scatter_dimension=1, tiled=True)]
    concatenate x4 -> x0, other arithmetic: 17.6 us -> none  [apply_rope(): jnp.concatenate([first * cos_t - second * sin_t, second * cos_t + first *...]
    psum x1 -> x0, blocking collectives: 13.9 us -> none  [local_block(): grad_norm_w = lax.psum(grad_norm_part, 'tp')]
    reduce_sum x3 -> x0, other arithmetic: 11 us -> none  [the longest x1 7.33 us: local_block(): attn_probs = jax.nn.softmax(jnp.where(causal, scores, -1e+30), axis=-1)]
  transfers between devices with their start and end apart: 5 -> 0, of which waited for: 5 -> 0; matrix products, arithmetic and copies ran while one was open for 22% -> 0% of each run, Pallas kernels for 0% -> 0%
where the time goes in v2:
time: 181 us
  Pallas kernels  173 us (96%)
  local copies, waits for them, and re-layouts  4.49 us (2%)
  other arithmetic  3.32 us (2%)
    pallas_call x1, Pallas kernels, local_block(): pl.pallas_call(functools.partial(block_kernel, size, stride), out_shape=[...  161 us
    pallas_call x1, Pallas kernels, local_block(): pl.pallas_call(weight_kernel, grid=(width // COLS,), out_shape=[shape((wi...  11.4 us
    unnamed x12, local copies, waits for them, and re-layouts  4.49 us

profile of v2, /device:TPU:81, one launch (start us, length us, event | category | flops | bytes accessed | tf_op | source)
XLA Modules:
  0.0 181.0 jit_solution(13476083511680144117)
XLA Ops:
  0.6 0.7 convert_element_type.10
  1.4 1.3 broadcast_add_fusion
  2.6 1.3 broadcast_multiply_fusion.angle_ref
  4.0 161.1 %attention_block.1 = (bf16[256,2048]{1,0:T(8,128)(2,1)}, bf16[256,2048]{1,0:T(8,128)(2,1)}, f32[256,2048]{1,0:T(8,128)}, f32[16,128]{1,0:T(8,128)}, bf16[2048,20...) custom-call(bf16[256,2048]{1,0:T(8,128)(2,1)} %bitcast.10, ...), custom_call_target="tpu_custom_call" | custom-call | tf_op jit(solution)/shard_map/attention_block/pallas_call | solution.py:616
  165.1 0.0 copy-start.2
  165.1 11.4 %weight_grads.1 = (f32[2048,256]{1,0:T(8,128)}, f32[2048,256]{1,0:T(8,128)}, f32[2048,256]{1,0:T(8,128)}) custom-call(bf16[2048,2048]{1,0:T(8,128)(2,1)} %get-tuple-element.19.a_ref, bf16[2048,256]{1,0:T(8,128)(2,1)} %get-tuple-element.20.dq_ref, bf16[2048,512]{1,0:T(8,128)(2,1)} %get-tuple-element.21.dkv_ref), custom_call_target="tpu_custom_call" | custom-call | tf_op jit(solution)/shard_map/weight_grads/pallas_call | solution.py:636
  176.5 0.0 copy-start.1
  176.5 0.0 copy-done.2
  176.5 0.0 copy-start
  176.5 1.0 copy.19
  177.5 0.6 copy-done.1
  178.1 1.0 copy.20
  179.1 0.0 copy-done
  179.1 0.0 copy-start.3
  179.1 1.3 copy.21
  180.4 0.0 copy-done.3
  180.4 0.6 copy.22
  (1 shorter events, 0.0 us)
Async XLA Ops:
  165.1 11.4 %copy-start.2 = (bf16[256,2048]{1,0:T(8,128)(2,1)S(1)}, bf16[256,2048]{1,0:T(8,128)(2,1)}, u32[]{:S(2)}) copy-start(bf16[256,2048]{1,0:T(8,128)(2,1)} %get-tuple-element.17) | copy-start | bytes 3145732
  176.5 1.6 copy-start.1
  176.5 2.6 %copy-start = (f32[256,2048]{1,0:T(8,128)S(1)}, f32[256,2048]{1,0:T(8,128)}, u32[]{:S(2)}) copy-start(f32[256,2048]{1,0:T(8,128)} %get-tuple-element.37) | copy-start | bytes 6291460
  179.1 1.3 copy-start.3

commit v3 on v2

--- a/solution.py
+++ b/solution.py
@@ -280,9 +280,9 @@
             remote(ref, ref, self.ssem.at[k], self.rsem.at[k], self.place.sib).wait_send()
 
 
-def block_kernel(size, stride, x_ref, dout_ref, gain_ref, angle_ref, wq_hbm, wk_hbm, wv_hbm, wo_hbm,
+def block_kernel(size, stride, norm_ref, pos_ref, freq_ref, x_hbm, dout_hbm, wq_hbm, wk_hbm, wv_hbm, wo_hbm,
                  out_ref, dx_ref, dwo_out, dw_ref, a_out, dq_out, dkv_out, wo_full, wq_full,
-                 act_full, big, wbuf, wo, wqt, q_ref, k_ref, v_ref, o_ref, dq_ref, dkv_ref, dkv_full, o_all, dq_all,
+                 x_ref, dout_ref, gain_ref, act_full, big, wbuf, wo, wqt, q_ref, k_ref, v_ref, o_ref, dq_ref, dkv_ref, dkv_full, o_all, dq_all,
                  relay_o, relay_q, lse_ref, cos_ref, sin_ref, m_scr, l_scr, acc,
                  d2d, sums, top, bot, from_l, from_r, wide, dw_me, dw_all, lsem,
                  ss_a, rs_a, ss_d, rs_d, ss_wo, rs_wo, ss_wq, rs_wq, ss_kv, rs_kv, ss_yo, rs_yo, ss_yq, rs_yq,
@@ -301,10 +301,14 @@
     for to in [{'tp': peer} for peer in peers] + [{'dp': p.group_z}, {'dp': p.group_y}]:
         pl.semaphore_signal(barrier, inc=1, device_id=to, device_id_type=MESH)
 
-    loads = [pltpu.make_async_copy(src, dst, lsem.at[i]) for i, (src, dst) in enumerate(
-        ((wq_hbm, wbuf.at[0]), (wo_hbm, wo), (wk_hbm, wbuf.at[1]), (wv_hbm, wbuf.at[2])))]
-    for copy in loads:
+    load_x, load_wq, load_wo, load_dout, *load_kv = [pltpu.make_async_copy(src, dst, lsem.at[i]) for i, (src, dst) in enumerate(
+        ((x_hbm, x_ref), (wq_hbm, wbuf.at[0]), (wo_hbm, wo), (dout_hbm, dout_ref), (wk_hbm, wbuf.at[1]), (wv_hbm, wbuf.at[2])))]
+    for copy in (load_x, load_wq, load_wo, load_dout, *load_kv):
         copy.start()
+    lanes = 128
+    groups = [slice(t * lanes, (t + 1) * lanes) for t in range(width // lanes)]
+    for t, cols in enumerate(groups):
+        gain_ref[:, cols] = 1.0 + norm_ref[t:t + 1, :]
 
     def weight_at(full):
         quarter = part_rows // 2
@@ -335,25 +339,27 @@
     dq_x = Exchange(p, block, dq_ref, dq_all, relay_q, ss_q, rs_q)
     kv_r = Scatter(p, block, dkv_ref, d2d, sums, top, bot, from_l, from_r, ss_r, rs_r)
 
-    def start_weight(g, shard, sem):
+    def start_weight(g, shard, src, sem):
         quarter = part_rows // 2
+        g.start([src.at[p.part, pl.ds(h * quarter, quarter)] for h in (0, 1)], src.at[p.part])
         own = pltpu.make_async_copy(shard.at[p.part], g.own_all, lsem.at[sem])
         own.start()
-        g.start([shard.at[p.part, pl.ds(h * quarter, quarter)] for h in (0, 1)], shard.at[p.part])
         return own
 
-    loads[1].wait()
-    loads[0].wait()
     pl.semaphore_wait(barrier, size + 1)
-    own_wo = start_weight(wo_g, wo, 4)
-
-    @pl.loop(0, parts)
+    load_wo.wait()
+    own_wo = start_weight(wo_g, wo, wo_hbm, 6)
+    load_wq.wait()
+
+    @pl.loop(0, width // COLS)
     def _(n):
         rows = pl.ds(pl.multiple_of(n * COLS, COLS), COLS)
         flipped = wbuf[0, rows, :].T
         for g in range(parts):
             wqt[g, :, rows] = flipped[g * part_rows:(g + 1) * part_rows, :]
-    own_wq = start_weight(wq_g, wqt, 5)
+    own_wq = start_weight(wq_g, wqt, wqt, 7)
+
+    load_x.wait()
 
     @pl.loop(0, block // 64)
     def _(n):
@@ -366,15 +372,17 @@
         g.first()
     act.start()
 
-    @pl.loop(0, seq // 64)
+    @pl.loop(0, seq // lanes)
     def _(n):
-        rows = pl.ds(pl.multiple_of(n * 64, 64), 64)
-        angle = angle_ref[rows, :]
+        rows = pl.ds(pl.multiple_of(n * lanes, lanes), lanes)
+        angle = jnp.broadcast_to(pos_ref[:, rows].astype(F32), (lanes, lanes)).T * freq_ref[...]
         cos_ref[rows, :] = jnp.cos(angle)
         sin_ref[rows, :] = jnp.sin(angle)
 
-    loads[2].wait()
-    loads[3].wait()
+    load_dout.wait()
+    big[p.chip, p.core] = dout_ref[...]
+    for copy in load_kv:
+        copy.wait()
 
     def project(first, second):
         @pl.loop(0, 2)
@@ -398,7 +406,6 @@
     project(p.me, p.sib)
     act.first()
     grad.start([dout_ref.at[pl.ds(h * (parts // 2), parts // 2)] for h in (0, 1)], dout_ref)
-    big[p.chip, p.core] = dout_ref[...]
     act.second()
     project(p.left, p.right)
     act.sibling_near()
@@ -406,7 +413,7 @@
     act.third()
     act.sibling_far()
     project(p.chip_o * 2 + p.core, p.chip_o * 2 + 1 - p.core)
-    a_copy = pltpu.make_async_copy(act_full, a_out, lsem.at[6])
+    a_copy = pltpu.make_async_copy(act_full, a_out, lsem.at[8])
     a_copy.start()
 
     row_ids = lax.broadcasted_iota(jnp.int32, (TILE, TILE), 0)
@@ -414,33 +421,42 @@
 
     def tile_rows(j):
         return pl.ds(pl.multiple_of(j * TILE, TILE), TILE)
+
+    def lane_groups(v):
+        return [v[:, t * lanes:(t + 1) * lanes] for t in range(TILE // lanes)]
+
+    def spread(v):
+        return jnp.concatenate([v] * (TILE // lanes), axis=-1)
+
+    diagonal = row_ids >= col_ids
 
     @pl.loop(0, seq // TILE)
     def _(i):
         rows = tile_rows(i)
         m_scr[...] = jnp.full(m_scr.shape, -1e30, F32)
+
+        def score(j, s):
+            dkv_ref[tile_rows(j), :] = s
+            m_scr[...] = functools.reduce(jnp.maximum, lane_groups(s), m_scr[...])
+
+        @pl.loop(0, i)
+        def _(j):
+            score(j, dot_nt(q_ref[rows, :], k_ref[tile_rows(j), :]))
+
+        score(i, jnp.where(diagonal, dot_nt(q_ref[rows, :], k_ref[rows, :]), -1e30))
+        m_scr[...] = jnp.broadcast_to(jnp.max(m_scr[...], axis=-1, keepdims=True), m_scr.shape)
         l_scr[...] = jnp.zeros(l_scr.shape, F32)
         acc[...] = jnp.zeros(acc.shape, F32)
 
         @pl.loop(0, i + 1)
         def _(j):
-            s = dot_nt(q_ref[rows, :], k_ref[tile_rows(j), :])
-            s = jnp.where(row_ids + (i - j) * TILE >= col_ids, s, -1e30)
-            dkv_ref[tile_rows(j), :] = s
-            m_old = m_scr[:, :1]
-            m_new = jnp.maximum(m_old, jnp.max(s, axis=-1, keepdims=True))
-            l_new = l_scr[:, :1] * jnp.exp(m_old - m_new) + jnp.sum(jnp.exp(s - m_new), axis=-1, keepdims=True)
-            m_scr[...] = jnp.broadcast_to(m_new, m_scr.shape)
-            l_scr[...] = jnp.broadcast_to(l_new, l_scr.shape)
-
-        lse_ref[rows, :] = m_scr[...] + jnp.log(l_scr[...])
-
-        @pl.loop(0, i + 1)
-        def _(j):
-            prob = jnp.exp(dkv_ref[tile_rows(j), :] - lse_ref[rows, :1]).astype(BF16)
-            acc[...] += dot_nn(prob, v_ref[tile_rows(j), :])
-
-        o_ref[rows, :] = acc[...].astype(BF16)
+            prob = jnp.exp(dkv_ref[tile_rows(j), :] - spread(m_scr[...]))
+            l_scr[...] = functools.reduce(jnp.add, lane_groups(prob), l_scr[...])
+            acc[...] += dot_nn(prob.astype(BF16), v_ref[tile_rows(j), :])
+
+        total = jnp.sum(l_scr[...], axis=-1, keepdims=True)
+        lse_ref[rows, :] = m_scr[...] + jnp.log(total)
+        o_ref[rows, :] = (acc[...] / total).astype(BF16)
 
     dkv_ref[...] = jnp.zeros(dkv_ref.shape, F32)
 
@@ -451,20 +467,24 @@
             rows = tile_rows(i)
             do = dot_nt(big[i].reshape(TILE, width), wo_rows()).astype(BF16)
             row_dot = jnp.sum(do.astype(F32) * o_ref[rows, :].astype(F32), axis=-1, keepdims=True)
+            m_scr[...] = jnp.broadcast_to(row_dot, m_scr.shape)
             acc[...] = jnp.zeros(acc.shape, F32)
             q = q_ref[rows, :]
 
-            @pl.loop(0, i + 1)
-            def _(j):
+            def inner(j, masked):
                 cols = tile_rows(j)
-                s = dot_nt(q, k_ref[cols, :])
-                prob = jnp.exp(s - lse_ref[rows, :1])
-                prob = jnp.where(row_ids + (i - j) * TILE >= col_ids, prob, 0.0)
+                prob = jnp.exp(dot_nt(q, k_ref[cols, :]) - spread(lse_ref[rows, :]))
+                if masked:
+                    prob = jnp.where(diagonal, prob, 0.0)
                 dkv_ref[cols, head:] += dot_tn(prob.astype(BF16), do)
-                dprob = dot_nt(do, v_ref[cols, :])
-                ds = (prob * (dprob - row_dot)).astype(BF16)
+                ds = (prob * (dot_nt(do, v_ref[cols, :]) - spread(m_scr[...]))).astype(BF16)
                 dkv_ref[cols, :head] += dot_tn(ds, q)
                 acc[...] += dot_nn(ds, k_ref[cols, :])
+
+            @pl.loop(0, i)
+            def _(j):
+                inner(j, False)
+            inner(i, True)
 
             dq_ref[rows, :] = rope(acc[...] * scale, cos_ref[rows, :], -sin_ref[rows, :]).astype(BF16)
 
@@ -480,14 +500,13 @@
     grad.third()
     grad.sibling_far()
     backward(p.chip_o, p.chip_o, 1)
-    dq_copy = pltpu.make_async_copy(dq_ref, dq_out, lsem.at[7])
+    dq_copy = pltpu.make_async_copy(dq_ref, dq_out, lsem.at[9])
     dq_copy.start()
 
     kv_r.chip_send()
     o_x.relay()
     kv_r.far()
     kv_r.near_first()
-    dq_x.start()
     for s in (wo_s, wq_s):
         s.forward()
 
@@ -506,6 +525,7 @@
     wo_copy.start()
 
     kv_r.near_second()
+    dq_x.start()
     grad.finish()
     wo_g.sibling()
     wo_g.sibling_near()
@@ -513,7 +533,6 @@
     wo_s.finish()
     load_wo = pltpu.make_async_copy(wo_full, big, lsem.at[2])
     load_wo.start()
-    dq_x.relay()
     o_x.recv()
     load_wo.wait()
 
@@ -533,6 +552,7 @@
     total = kv_r.last()
     dkv_full[own, :head] = rope(total[:, :head], cos_ref[own, :], -sin_ref[own, :]).astype(BF16)
     dkv_full[own, head:] = total[:, head:].astype(BF16)
+    dq_x.relay()
     kv_g.start()
     dq_x.recv()
     wo_copy.wait()
@@ -561,9 +581,8 @@
         dout = dout_ref[n // per, pl.ds(pl.multiple_of(lax.rem(n, per) * sub, sub), sub), :].astype(F32)
         dx_ref[rows, :] = (dout + inv * (gn - normed * jnp.mean(gn * normed, axis=-1, keepdims=True))).astype(BF16)
 
-    lanes = 128
-    for t in range(width // lanes):
-        dw_all[0, t:t + 1, :] = dw_me[:, t * lanes:(t + 1) * lanes]
+    for t, cols in enumerate(groups):
+        dw_all[0, t:t + 1, :] = dw_me[:, cols]
     for d in range(1, size):
         remote(dw_all.at[0], dw_all.at[d], ss_w.at[d], rs_w.at[d], peers[d - 1]).start()
     kv_g.second()
@@ -586,12 +605,19 @@
     kv_copy.wait()
 
 
-def weight_kernel(a_ref, dq_ref, dkv_ref, dwq_ref, dwk_ref, dwv_ref):
+def weight_kernel(a_ref, dq_ref, dkv_ref, out_in, dx_in, dwo_in, dw_in,
+                  dwq_ref, dwk_ref, dwv_ref, out_ref, dx_ref, dwo_ref, dw_ref, flipped):
     head = dq_ref.shape[1]
-    a = a_ref[...]
-    dwq_ref[...] = dot_tn(dq_ref[...], a).T
-    dwk_ref[...] = dot_tn(dkv_ref[:, :head], a).T
-    dwv_ref[...] = dot_tn(dkv_ref[:, head:], a).T
+
+    @pl.when(pl.program_id(0) == 0)
+    def _():
+        flipped[:head, :] = dq_ref[...].T
+        flipped[head:, :] = dkv_ref[...].T
+
+    for src, dst in ((out_in, out_ref), (dx_in, dx_ref), (dwo_in, dwo_ref), (dw_in, dw_ref)):
+        dst[...] = src[...]
+    for n, dst in enumerate((dwq_ref, dwk_ref, dwv_ref)):
+        dst[...] = dot_nn(flipped[n * head:(n + 1) * head, :], a_ref[...]).T
 
 
 def local_block(size, stride, hidden, positions, norm_w, w_query, w_key, w_value, w_out, grad_out):
@@ -601,10 +627,9 @@
     half = head // 2
     chips, parts = size // 2, 4
     part_rows = block // parts
+    lanes = 128
     x, dout = hidden[0], grad_out[0].reshape(parts, part_rows, width)
-    gain = (1.0 + norm_w)[None, :]
-    inv_freq = 10000.0 ** (-2.0 * jnp.arange(half, dtype=F32) / head)
-    angle = positions[0].astype(F32)[:, None] * inv_freq
+    inv_freq = (10000.0 ** (-2.0 * jnp.arange(half, dtype=F32) / head))[None, :]
     vm = pl.BlockSpec(memory_space=pltpu.VMEM)
     hbm = pl.BlockSpec(memory_space=pl.ANY)
     dma = pltpu.SemaphoreType.DMA
@@ -618,30 +643,37 @@
         out_shape=[shape((block, width), BF16)] * 2 + [shape((head, width), F32), shape((width // 128, 128), F32),
                                                        shape((seq, width), BF16), shape((seq, head), BF16),
                                                        shape((seq, kv), BF16), shape(full, BF16), shape(full, BF16)],
-        in_specs=[vm] * 4 + [hbm] * 4,
+        in_specs=[vm] * 3 + [hbm] * 6,
         out_specs=[vm, vm, hbm, vm] + [hbm] * 5,
-        scratch_shapes=[V((seq, width), BF16), V(full, BF16), V((3, width, head), BF16), V((parts, part_rows, width), BF16),
+        scratch_shapes=[V((block, width), BF16), V((parts, part_rows, width), BF16), V((1, width), F32),
+                        V((seq, width), BF16), V(full, BF16), V((3, width, head), BF16), V((parts, part_rows, width), BF16),
                         V((parts, part_rows, width), BF16)] + [V((seq, head), BF16)] * 5
         + [V((seq, kv), F32), V((seq, kv), BF16), V((size, block, head), BF16), V((size, block, head), BF16),
            V((2, block, head), BF16), V((2, block, head), BF16), V((seq, 128), F32), V((seq, half), F32), V((seq, half), F32),
            V((TILE, 128), F32), V((TILE, 128), F32), V((TILE, head), F32),
            V((4, block, kv), F32), V((3, block, kv), F32), V((block // 2, kv), F32), V((block // 2, kv), F32),
            V((block, kv), F32), V((block, kv), F32), V((head, width), F32), V((1, width), F32),
-           V((size, width // 128, 128), F32), dma((8,))]
+           V((size, width // 128, 128), F32), dma((10,))]
         + [dma((13,))] * 10 + [dma((8,))] * 4 + [dma((9,))] * 4 + [dma((10,))] * 2 + [dma((size,))] * 2,
         compiler_params=pltpu.CompilerParams(collective_id=0, has_side_effects=True, vmem_limit_bytes=VMEM_LIMIT),
         name='attention_block',
-    )(x, dout, gain, angle, w_query, w_key, w_value, w_out.reshape(parts, part_rows, width))
-
-    dwq, dwk, dwv = pl.pallas_call(
+    )(norm_w.reshape(width // lanes, lanes), positions, inv_freq, x, dout, w_query, w_key, w_value,
+      w_out.reshape(parts, part_rows, width))
+
+    steps = width // COLS
+    whole = lambda *dims: pl.BlockSpec(dims, lambda n: (0, 0))
+    rows = lambda *dims: pl.BlockSpec(dims, lambda n: (n, 0))
+    small = (width // lanes, lanes)
+    passed = [rows(block // steps, width), rows(block // steps, width), rows(head // steps, width), whole(*small)]
+    dwq, dwk, dwv, out, dx, dwo, dw = pl.pallas_call(
         weight_kernel,
-        grid=(width // COLS,),
-        out_shape=[shape((width, head), F32)] * 3,
-        in_specs=[pl.BlockSpec((seq, COLS), lambda n: (0, n)), pl.BlockSpec((seq, head), lambda n: (0, 0)),
-                  pl.BlockSpec((seq, kv), lambda n: (0, 0))],
-        out_specs=[pl.BlockSpec((COLS, head), lambda n: (n, 0))] * 3,
+        grid=(steps,),
+        out_shape=[shape((width, head), F32)] * 3 + [shape((block, width), BF16)] * 2 + [shape((head, width), F32), shape(small, F32)],
+        in_specs=[pl.BlockSpec((seq, COLS), lambda n: (0, n)), whole(seq, head), whole(seq, kv)] + passed,
+        out_specs=[rows(COLS, head)] * 3 + passed,
+        scratch_shapes=[V((3 * head, seq), BF16)],
         name='weight_grads',
-    )(act, dq, dkv)
+    )(act, dq, dkv, out, dx, dwo, dw)
     return out[None], dx[None], dwq, dwo, dwk, dwv, dw.reshape(width)
 
 

time: 181 us -> 163 us (0.901)
  Pallas kernels: 173 us -> 161 us
  local copies, waits for them, and re-layouts: 4.49 us -> 0 us
  other arithmetic: 3.32 us -> 0.53 us
    pallas_call x1, Pallas kernels: 161 us -> 148 us  [local_block(): pl.pallas_call(functools.partial(block_kernel, size, stride), out_shape=[...]
    unnamed x12 -> x0, local copies, waits for them, and re-layouts: 4.49 us -> none
    pallas_call x1, Pallas kernels: 11.4 us -> 13.6 us  [local_block(): pl.pallas_call(weight_kernel, grid=(steps,), out_shape=[shape((width, hea...]
where the time goes in v3:
time: 163 us
  Pallas kernels  161 us (99%)
    pallas_call x1, Pallas kernels, local_block(): pl.pallas_call(functools.partial(block_kernel, size, stride), out_shape=[...  148 us
    pallas_call x1, Pallas kernels, local_block(): pl.pallas_call(weight_kernel, grid=(steps,), out_shape=[shape((width, hea...  13.6 us

profile of v3, /device:TPU:81, one launch (start us, length us, event | category | flops | bytes accessed | tf_op | source)
XLA Modules:
  0.0 162.8 jit_solution(2587169646865422819)
XLA Ops:
  0.6 0.5 multiply_power_fusion.freq_ref
  1.2 147.8 %attention_block.1 = (bf16[256,2048]{1,0:T(8,128)(2,1)}, bf16[256,2048]{1,0:T(8,128)(2,1)}, f32[256,2048]{1,0:T(8,128)}, f32[16,128]{1,0:T(8,128)}, bf16[2048,20...) custom-call(f32[16,128]{1,0:T(8,128)} %bitcast.10, ...), custom_call_target="tpu_custom_call" | custom-call | tf_op jit(solution)/shard_map/attention_block/pallas_call | solution.py:641
  149.0 13.6 %weight_grads.1 = (f32[2048,256]{1,0:T(8,128)}, f32[2048,256]{1,0:T(8,128)}, f32[2048,256]{1,0:T(8,128)}, bf16[256,2048]{1,0:T(8,128)(2,1)}, bf16[256,2048]{1,0:...) custom-call(bf16[2048,2048]{1,0:T(8,128)(2,1)} %get-tuple-element.21.a_ref, ...), custom_call_target="tpu_custom_call" | custom-call | tf_op jit(solution)/shard_map/weight_grads/pallas_call | solution.py:668

commit v4 on v3

--- a/solution.py
+++ b/solution.py
@@ -2,6 +2,7 @@
 
 import jax
 import jax.numpy as jnp
+import numpy as np
 from jax import lax
 from jax.experimental import pallas as pl
 from jax.experimental.pallas import tpu as pltpu
@@ -11,8 +12,10 @@
 F32 = jnp.float32
 BF16 = jnp.bfloat16
 TILE = 512
+STRIP = 256
 COLS = 512
 VMEM_LIMIT = 63 * 1024 * 1024
+KEPT = 16 * 1024 * 1024
 
 
 def dot_nn(a, b):
@@ -281,8 +284,8 @@
 
 
 def block_kernel(size, stride, norm_ref, pos_ref, freq_ref, x_hbm, dout_hbm, wq_hbm, wk_hbm, wv_hbm, wo_hbm,
-                 out_ref, dx_ref, dwo_out, dw_ref, a_out, dq_out, dkv_out, wo_full, wq_full,
-                 x_ref, dout_ref, gain_ref, act_full, big, wbuf, wo, wqt, q_ref, k_ref, v_ref, o_ref, dq_ref, dkv_ref, dkv_full, o_all, dq_all,
+                 out_ref, dx_ref, dwo_ref, dw_ref, act_full, dq_ref, dkv_full, wo_full, wq_full,
+                 x_ref, dout_ref, gain_ref, big, wbuf, wo, wqt, q_ref, k_ref, v_ref, o_ref, dkv_ref, o_all, dq_all,
                  relay_o, relay_q, lse_ref, cos_ref, sin_ref, m_scr, l_scr, acc,
                  d2d, sums, top, bot, from_l, from_r, wide, dw_me, dw_all, lsem,
                  ss_a, rs_a, ss_d, rs_d, ss_wo, rs_wo, ss_wq, rs_wq, ss_kv, rs_kv, ss_yo, rs_yo, ss_yq, rs_yq,
@@ -413,8 +416,6 @@
     act.third()
     act.sibling_far()
     project(p.chip_o * 2 + p.core, p.chip_o * 2 + 1 - p.core)
-    a_copy = pltpu.make_async_copy(act_full, a_out, lsem.at[8])
-    a_copy.start()
 
     row_ids = lax.broadcasted_iota(jnp.int32, (TILE, TILE), 0)
     col_ids = lax.broadcasted_iota(jnp.int32, (TILE, TILE), 1)
@@ -494,14 +495,25 @@
     o_x.start()
     for s in (wo_s, wq_s):
         s.relay()
+    act.finish()
+
+    def strip(n):
+        return pl.ds(pl.multiple_of(n * STRIP, STRIP), STRIP)
+
+    @pl.loop(0, width // STRIP)
+    def _(i):
+        @pl.loop(0, i + 1)
+        def _(j):
+            upper, lower = act_full[strip(j), strip(i)], act_full[strip(i), strip(j)]
+            act_full[strip(i), strip(j)] = upper.T
+            act_full[strip(j), strip(i)] = lower.T
+
     grad.second()
     grad.sibling_near()
     backward(p.chip_l, p.chip_r, 2)
     grad.third()
     grad.sibling_far()
     backward(p.chip_o, p.chip_o, 1)
-    dq_copy = pltpu.make_async_copy(dq_ref, dq_out, lsem.at[9])
-    dq_copy.start()
 
     kv_r.chip_send()
     o_x.relay()
@@ -519,10 +531,8 @@
         return big[:, :, :, :, cols].reshape(seq, COLS)
 
     def weight_o(cols):
-        wide[:, cols] = dot_tn(o_ref[...], big_cols(cols))
+        dwo_ref[:, cols] = dot_tn(o_ref[...], big_cols(cols))
     col_tiles(weight_o)
-    wo_copy = pltpu.make_async_copy(wide, dwo_out, lsem.at[1])
-    wo_copy.start()
 
     kv_r.near_second()
     dq_x.start()
@@ -555,7 +565,6 @@
     dq_x.relay()
     kv_g.start()
     dq_x.recv()
-    wo_copy.wait()
     load_wq.wait()
 
     def finish_da(cols):
@@ -593,31 +602,27 @@
     kv_g.sibling()
     kv_g.sibling_near()
     kv_g.sibling_far()
-    kv_copy = pltpu.make_async_copy(dkv_full, dkv_out, lsem.at[2])
-    kv_copy.start()
 
     for d in range(1, size):
         remote(dw_all.at[0], dw_all.at[0], ss_w.at[d], rs_w.at[d], p.sib).wait_send()
-    for g in (act, wo_g, wq_g, kv_g, kv_r, o_x, dq_x):
+    for g in (wo_g, wq_g, kv_g, kv_r, o_x, dq_x):
         g.finish()
-    a_copy.wait()
-    dq_copy.wait()
-    kv_copy.wait()
-
-
-def weight_kernel(a_ref, dq_ref, dkv_ref, out_in, dx_in, dwo_in, dw_in,
-                  dwq_ref, dwk_ref, dwv_ref, out_ref, dx_ref, dwo_ref, dw_ref, flipped):
+
+
+def weight_kernel(out_in, dx_in, dwo_in, dw_in, a_ref, dq_ref, dkv_ref,
+                  dwq_ref, dwk_ref, dwv_ref, out_ref, dx_ref, dwo_ref, dw_ref):
+    step = pl.program_id(0)
     head = dq_ref.shape[1]
 
-    @pl.when(pl.program_id(0) == 0)
-    def _():
-        flipped[:head, :] = dq_ref[...].T
-        flipped[head:, :] = dkv_ref[...].T
-
-    for src, dst in ((out_in, out_ref), (dx_in, dx_ref), (dwo_in, dwo_ref), (dw_in, dw_ref)):
-        dst[...] = src[...]
-    for n, dst in enumerate((dwq_ref, dwk_ref, dwv_ref)):
-        dst[...] = dot_nn(flipped[n * head:(n + 1) * head, :], a_ref[...]).T
+    def part(rows):
+        return pl.ds(pl.multiple_of(step * rows, rows), rows)
+    for src, dst in ((out_in, out_ref), (dx_in, dx_ref), (dwo_in, dwo_ref)):
+        dst[...] = src[part(dst.shape[0]), :]
+    dw_ref[...] = dw_in[...]
+    a = a_ref[part(dwq_ref.shape[0]), :]
+    dwq_ref[...] = dot_nn(a, dq_ref[...])
+    dwk_ref[...] = dot_nn(a, dkv_ref[:, :head])
+    dwv_ref[...] = dot_nn(a, dkv_ref[:, head:])
 
 
 def local_block(size, stride, hidden, positions, norm_w, w_query, w_key, w_value, w_out, grad_out):
@@ -629,7 +634,7 @@
     part_rows = block // parts
     lanes = 128
     x, dout = hidden[0], grad_out[0].reshape(parts, part_rows, width)
-    inv_freq = (10000.0 ** (-2.0 * jnp.arange(half, dtype=F32) / head))[None, :]
+    inv_freq = (10000.0 ** (-2.0 * np.arange(half) / head)).astype(np.float32)[None, :]
     vm = pl.BlockSpec(memory_space=pltpu.VMEM)
     hbm = pl.BlockSpec(memory_space=pl.ANY)
     dma = pltpu.SemaphoreType.DMA
@@ -637,25 +642,25 @@
     V = pltpu.VMEM
     full = (chips, 2, parts, part_rows, width)
     kv = 2 * head
-
-    out, dx, dwo, dw, act, dq, dkv, _, _ = pl.pallas_call(
+    small = (width // lanes, lanes)
+
+    *results, _, _ = pl.pallas_call(
         functools.partial(block_kernel, size, stride),
-        out_shape=[shape((block, width), BF16)] * 2 + [shape((head, width), F32), shape((width // 128, 128), F32),
-                                                       shape((seq, width), BF16), shape((seq, head), BF16),
-                                                       shape((seq, kv), BF16), shape(full, BF16), shape(full, BF16)],
+        out_shape=[V((block, width), BF16), V((block, width), BF16), V((head, width), F32), V(small, F32),
+                   V((seq, width), BF16), V((seq, head), BF16), V((seq, kv), BF16), shape(full, BF16), shape(full, BF16)],
         in_specs=[vm] * 3 + [hbm] * 6,
-        out_specs=[vm, vm, hbm, vm] + [hbm] * 5,
+        out_specs=[vm] * 7 + [hbm] * 2,
         scratch_shapes=[V((block, width), BF16), V((parts, part_rows, width), BF16), V((1, width), F32),
-                        V((seq, width), BF16), V(full, BF16), V((3, width, head), BF16), V((parts, part_rows, width), BF16),
-                        V((parts, part_rows, width), BF16)] + [V((seq, head), BF16)] * 5
-        + [V((seq, kv), F32), V((seq, kv), BF16), V((size, block, head), BF16), V((size, block, head), BF16),
+                        V(full, BF16), V((3, width, head), BF16), V((parts, part_rows, width), BF16),
+                        V((parts, part_rows, width), BF16)] + [V((seq, head), BF16)] * 4
+        + [V((seq, kv), F32), V((size, block, head), BF16), V((size, block, head), BF16),
            V((2, block, head), BF16), V((2, block, head), BF16), V((seq, 128), F32), V((seq, half), F32), V((seq, half), F32),
            V((TILE, 128), F32), V((TILE, 128), F32), V((TILE, head), F32),
            V((4, block, kv), F32), V((3, block, kv), F32), V((block // 2, kv), F32), V((block // 2, kv), F32),
            V((block, kv), F32), V((block, kv), F32), V((head, width), F32), V((1, width), F32),
-           V((size, width // 128, 128), F32), dma((10,))]
+           V((size, width // 128, 128), F32), dma((8,))]
         + [dma((13,))] * 10 + [dma((8,))] * 4 + [dma((9,))] * 4 + [dma((10,))] * 2 + [dma((size,))] * 2,
-        compiler_params=pltpu.CompilerParams(collective_id=0, has_side_effects=True, vmem_limit_bytes=VMEM_LIMIT),
+        compiler_params=pltpu.CompilerParams(collective_id=0, has_side_effects=True, vmem_limit_bytes=VMEM_LIMIT - KEPT),
         name='attention_block',
     )(norm_w.reshape(width // lanes, lanes), positions, inv_freq, x, dout, w_query, w_key, w_value,
       w_out.reshape(parts, part_rows, width))
@@ -663,17 +668,16 @@
     steps = width // COLS
     whole = lambda *dims: pl.BlockSpec(dims, lambda n: (0, 0))
     rows = lambda *dims: pl.BlockSpec(dims, lambda n: (n, 0))
-    small = (width // lanes, lanes)
     passed = [rows(block // steps, width), rows(block // steps, width), rows(head // steps, width), whole(*small)]
     dwq, dwk, dwv, out, dx, dwo, dw = pl.pallas_call(
         weight_kernel,
         grid=(steps,),
         out_shape=[shape((width, head), F32)] * 3 + [shape((block, width), BF16)] * 2 + [shape((head, width), F32), shape(small, F32)],
-        in_specs=[pl.BlockSpec((seq, COLS), lambda n: (0, n)), whole(seq, head), whole(seq, kv)] + passed,
+        in_specs=[vm] * 7,
         out_specs=[rows(COLS, head)] * 3 + passed,
-        scratch_shapes=[V((3 * head, seq), BF16)],
+        compiler_params=pltpu.CompilerParams(vmem_limit_bytes=VMEM_LIMIT - KEPT),
         name='weight_grads',
-    )(act, dq, dkv, out, dx, dwo, dw)
+    )(*[pltpu.with_memory_space_constraint(v, V) for v in results])
     return out[None], dx[None], dwq, dwo, dwk, dwv, dw.reshape(width)
 
 

time: 163 us -> 155 us (0.951)
  Pallas kernels: 161 us -> 154 us
    pallas_call x1, Pallas kernels: 13.6 us -> 8.78 us  [local_block(): pl.pallas_call(weight_kernel, grid=(steps,), out_shape=[shape((width, hea...]
    pallas_call x1, Pallas kernels: 148 us -> 146 us  [local_block(): pl.pallas_call(functools.partial(block_kernel, size, stride), out_shape=[...]
where the time goes in v4:
time: 155 us
  Pallas kernels  154 us (99%)
    pallas_call x1, Pallas kernels, local_block(): pl.pallas_call(functools.partial(block_kernel, size, stride), out_shape=[...  146 us
    pallas_call x1, Pallas kernels, local_block(): pl.pallas_call(weight_kernel, grid=(steps,), out_shape=[shape((width, hea...  8.78 us

profile of v4, /device:TPU:81, one launch (start us, length us, event | category | flops | bytes accessed | tf_op | source)
XLA Modules:
  0.0 155.1 jit_solution(15758142789399482445)
XLA Ops:
  0.6 145.6 %attention_block.1 = (bf16[256,2048]{1,0:T(8,128)(2,1)S(1)}, bf16[256,2048]{1,0:T(8,128)(2,1)S(1)}, f32[256,2048]{1,0:T(8,128)S(1)}, f32[16,128]{1,0:T(8,128)S(1...) custom-call(f32[16,128]{1,0:T(8,128)} %bitcast.10, ...), custom_call_target="tpu_custom_call" | custom-call | tf_op jit(solution)/shard_map/attention_block/pallas_call | solution.py:647
  146.3 8.8 %weight_grads.1 = (f32[2048,256]{1,0:T(8,128)}, f32[2048,256]{1,0:T(8,128)}, f32[2048,256]{1,0:T(8,128)}, bf16[256,2048]{1,0:T(8,128)(2,1)}, bf16[256,2048]{1,0:...) custom-call(bf16[256,2048]{1,0:T(8,128)(2,1)S(1)} %get-tuple-element.21.out_in, ...), custom_call_target="tpu_custom_call" | custom-call | tf_op jit(solution)/shard_map/weight_grads/pallas_call | solution.py:672

commit v5 on v4

--- a/solution.py
+++ b/solution.py
@@ -284,8 +284,8 @@
 
 
 def block_kernel(size, stride, norm_ref, pos_ref, freq_ref, x_hbm, dout_hbm, wq_hbm, wk_hbm, wv_hbm, wo_hbm,
-                 out_ref, dx_ref, dwo_ref, dw_ref, act_full, dq_ref, dkv_full, wo_full, wq_full,
-                 x_ref, dout_ref, gain_ref, big, wbuf, wo, wqt, q_ref, k_ref, v_ref, o_ref, dkv_ref, o_all, dq_all,
+                 out_ref, dx_ref, dwo_ref, dwq_ref, dw_ref, act_full, dkv_full, wo_full, wq_full,
+                 x_ref, dout_ref, gain_ref, big, wbuf, wo, wqt, q_ref, k_ref, v_ref, o_ref, dq_ref, dkv_ref, o_all, dq_all,
                  relay_o, relay_q, lse_ref, cos_ref, sin_ref, m_scr, l_scr, acc,
                  d2d, sums, top, bot, from_l, from_r, wide, dw_me, dw_all, lsem,
                  ss_a, rs_a, ss_d, rs_d, ss_wo, rs_wo, ss_wq, rs_wq, ss_kv, rs_kv, ss_yo, rs_yo, ss_yq, rs_yq,
@@ -543,6 +543,10 @@
     wo_s.finish()
     load_wo = pltpu.make_async_copy(wo_full, big, lsem.at[2])
     load_wo.start()
+
+    def weight_q(cols):
+        dwq_ref[cols, :] = dot_nn(act_full[cols, :], dq_ref[...])
+    col_tiles(weight_q)
     o_x.recv()
     load_wo.wait()
 
@@ -591,13 +595,14 @@
         dx_ref[rows, :] = (dout + inv * (gn - normed * jnp.mean(gn * normed, axis=-1, keepdims=True))).astype(BF16)
 
     for t, cols in enumerate(groups):
-        dw_all[0, t:t + 1, :] = dw_me[:, cols]
+        dw_all[p.me, t:t + 1, :] = dw_me[:, cols]
     for d in range(1, size):
-        remote(dw_all.at[0], dw_all.at[d], ss_w.at[d], rs_w.at[d], peers[d - 1]).start()
+        remote(dw_all.at[p.me], dw_all.at[p.me], ss_w.at[d], rs_w.at[d], peers[d - 1]).start()
     kv_g.second()
     kv_g.third()
     for d in range(1, size):
-        remote(dw_all.at[d], dw_all.at[d], ss_w.at[d], rs_w.at[d], p.sib).wait_recv()
+        source = dw_all.at[lax.rem(p.me + size - d, size)]
+        remote(source, source, ss_w.at[d], rs_w.at[d], p.sib).wait_recv()
     dw_ref[...] = jnp.sum(dw_all[...], axis=0)
     kv_g.sibling()
     kv_g.sibling_near()
@@ -609,18 +614,17 @@
         g.finish()
 
 
-def weight_kernel(out_in, dx_in, dwo_in, dw_in, a_ref, dq_ref, dkv_ref,
-                  dwq_ref, dwk_ref, dwv_ref, out_ref, dx_ref, dwo_ref, dw_ref):
+def weight_kernel(out_in, dx_in, dwo_in, dwq_in, dw_in, a_ref, dkv_ref,
+                  dwk_ref, dwv_ref, out_ref, dx_ref, dwo_ref, dwq_ref, dw_ref):
     step = pl.program_id(0)
-    head = dq_ref.shape[1]
+    head = dwk_ref.shape[1]
 
     def part(rows):
         return pl.ds(pl.multiple_of(step * rows, rows), rows)
-    for src, dst in ((out_in, out_ref), (dx_in, dx_ref), (dwo_in, dwo_ref)):
+    for src, dst in ((out_in, out_ref), (dx_in, dx_ref), (dwo_in, dwo_ref), (dwq_in, dwq_ref)):
         dst[...] = src[part(dst.shape[0]), :]
     dw_ref[...] = dw_in[...]
-    a = a_ref[part(dwq_ref.shape[0]), :]
-    dwq_ref[...] = dot_nn(a, dq_ref[...])
+    a = a_ref[part(dwk_ref.shape[0]), :]
     dwk_ref[...] = dot_nn(a, dkv_ref[:, :head])
     dwv_ref[...] = dot_nn(a, dkv_ref[:, head:])
 
@@ -646,13 +650,13 @@
 
     *results, _, _ = pl.pallas_call(
         functools.partial(block_kernel, size, stride),
-        out_shape=[V((block, width), BF16), V((block, width), BF16), V((head, width), F32), V(small, F32),
-                   V((seq, width), BF16), V((seq, head), BF16), V((seq, kv), BF16), shape(full, BF16), shape(full, BF16)],
+        out_shape=[V((block, width), BF16), V((block, width), BF16), V((head, width), F32), V((width, head), F32), V(small, F32),
+                   V((seq, width), BF16), V((seq, kv), BF16), shape(full, BF16), shape(full, BF16)],
         in_specs=[vm] * 3 + [hbm] * 6,
         out_specs=[vm] * 7 + [hbm] * 2,
         scratch_shapes=[V((block, width), BF16), V((parts, part_rows, width), BF16), V((1, width), F32),
                         V(full, BF16), V((3, width, head), BF16), V((parts, part_rows, width), BF16),
-                        V((parts, part_rows, width), BF16)] + [V((seq, head), BF16)] * 4
+                        V((parts, part_rows, width), BF16)] + [V((seq, head), BF16)] * 5
         + [V((seq, kv), F32), V((size, block, head), BF16), V((size, block, head), BF16),
            V((2, block, head), BF16), V((2, block, head), BF16), V((seq, 128), F32), V((seq, half), F32), V((seq, half), F32),
            V((TILE, 128), F32), V((TILE, 128), F32), V((TILE, head), F32),
@@ -668,13 +672,15 @@
     steps = width // COLS
     whole = lambda *dims: pl.BlockSpec(dims, lambda n: (0, 0))
     rows = lambda *dims: pl.BlockSpec(dims, lambda n: (n, 0))
-    passed = [rows(block // steps, width), rows(block // steps, width), rows(head // steps, width), whole(*small)]
-    dwq, dwk, dwv, out, dx, dwo, dw = pl.pallas_call(
+    passed = [rows(block // steps, width), rows(block // steps, width), rows(head // steps, width), rows(width // steps, head),
+              whole(*small)]
+    dwk, dwv, out, dx, dwo, dwq, dw = pl.pallas_call(
         weight_kernel,
         grid=(steps,),
-        out_shape=[shape((width, head), F32)] * 3 + [shape((block, width), BF16)] * 2 + [shape((head, width), F32), shape(small, F32)],
+        out_shape=[shape((width, head), F32)] * 2 + [shape((block, width), BF16)] * 2
+        + [shape((head, width), F32), shape((width, head), F32), shape(small, F32)],
         in_specs=[vm] * 7,
-        out_specs=[rows(COLS, head)] * 3 + passed,
+        out_specs=[rows(width // steps, head)] * 2 + passed,
         compiler_params=pltpu.CompilerParams(vmem_limit_bytes=VMEM_LIMIT - KEPT),
         name='weight_grads',
     )(*[pltpu.with_memory_space_constraint(v, V) for v in results])

time: 155 us -> 153 us (0.987)
  Pallas kernels: 154 us -> 152 us
    pallas_call x1, Pallas kernels: 8.78 us -> 6.64 us  [local_block(): pl.pallas_call(weight_kernel, grid=(steps,), out_shape=[shape((width, hea...]
where the time goes in v5:
time: 153 us
  Pallas kernels  152 us (99%)
    pallas_call x1, Pallas kernels, local_block(): pl.pallas_call(functools.partial(block_kernel, size, stride), out_shape=[...  146 us
    pallas_call x1, Pallas kernels, local_block(): pl.pallas_call(weight_kernel, grid=(steps,), out_shape=[shape((width, hea...  6.64 us

profile of v5, /device:TPU:81, one launch (start us, length us, event | category | flops | bytes accessed | tf_op | source)
XLA Modules:
  0.0 153.0 jit_solution(610580546806830675)
XLA Ops:
  0.6 145.6 %attention_block.1 = (bf16[256,2048]{1,0:T(8,128)(2,1)S(1)}, bf16[256,2048]{1,0:T(8,128)(2,1)S(1)}, f32[256,2048]{1,0:T(8,128)S(1)}, f32[2048,256]{1,0:T(8,128)S...) custom-call(f32[16,128]{1,0:T(8,128)} %bitcast.10, ...), custom_call_target="tpu_custom_call" | custom-call | tf_op jit(solution)/shard_map/attention_block/pallas_call | solution.py:651
  146.3 6.6 %weight_grads.1 = (f32[2048,256]{1,0:T(8,128)}, f32[2048,256]{1,0:T(8,128)}, bf16[256,2048]{1,0:T(8,128)(2,1)}, bf16[256,2048]{1,0:T(8,128)(2,1)}, f32[256,2048]...) custom-call(bf16[256,2048]{1,0:T(8,128)(2,1)S(1)} %get-tuple-element.21.out_in, ...), custom_call_target="tpu_custom_call" | custom-call | tf_op jit(solution)/shard_map/weight_grads/pallas_call | solution.py:677

commit v6 on v5

--- a/solution.py
+++ b/solution.py
@@ -283,11 +283,11 @@
             remote(ref, ref, self.ssem.at[k], self.rsem.at[k], self.place.sib).wait_send()
 
 
-def block_kernel(size, stride, norm_ref, pos_ref, freq_ref, x_hbm, dout_hbm, wq_hbm, wk_hbm, wv_hbm, wo_hbm,
+def block_kernel(size, stride, norm_hbm, pos_hbm, freq_hbm, x_hbm, dout_hbm, wq_hbm, wk_hbm, wv_hbm, wo_hbm,
                  out_ref, dx_ref, dwo_ref, dwq_ref, dw_ref, act_full, dkv_full, wo_full, wq_full,
-                 x_ref, dout_ref, gain_ref, big, wbuf, wo, wqt, q_ref, k_ref, v_ref, o_ref, dq_ref, dkv_ref, o_all, dq_all,
+                 norm_ref, pos_ref, freq_ref, x_ref, dout_ref, gain_ref, big, wbuf, wo, wqt, q_ref, k_ref, v_ref, o_ref, dq_ref, dkv_ref, o_all, dq_all,
                  relay_o, relay_q, lse_ref, cos_ref, sin_ref, m_scr, l_scr, acc,
-                 d2d, sums, top, bot, from_l, from_r, wide, dw_me, dw_all, lsem,
+                 d2d, sums, top, bot, from_l, from_r, wide, dw_me, dw_all, lsem, ssem,
                  ss_a, rs_a, ss_d, rs_d, ss_wo, rs_wo, ss_wq, rs_wq, ss_kv, rs_kv, ss_yo, rs_yo, ss_yq, rs_yq,
                  ss_o, rs_o, ss_q, rs_q, ss_r, rs_r, ss_w, rs_w):
     p = Place(size, stride)
@@ -306,8 +306,12 @@
 
     load_x, load_wq, load_wo, load_dout, *load_kv = [pltpu.make_async_copy(src, dst, lsem.at[i]) for i, (src, dst) in enumerate(
         ((x_hbm, x_ref), (wq_hbm, wbuf.at[0]), (wo_hbm, wo), (dout_hbm, dout_ref), (wk_hbm, wbuf.at[1]), (wv_hbm, wbuf.at[2])))]
-    for copy in (load_x, load_wq, load_wo, load_dout, *load_kv):
+    small = [pltpu.make_async_copy(src, dst, ssem.at[i]) for i, (src, dst) in enumerate(
+        ((norm_hbm, norm_ref), (pos_hbm, pos_ref), (freq_hbm, freq_ref)))]
+    for copy in (*small, load_x, load_wq, load_wo, load_dout, *load_kv):
         copy.start()
+    for copy in small:
+        copy.wait()
     lanes = 128
     groups = [slice(t * lanes, (t + 1) * lanes) for t in range(width // lanes)]
     for t, cols in enumerate(groups):
@@ -615,18 +619,24 @@
 
 
 def weight_kernel(out_in, dx_in, dwo_in, dwq_in, dw_in, a_ref, dkv_ref,
-                  dwk_ref, dwv_ref, out_ref, dx_ref, dwo_ref, dwq_ref, dw_ref):
-    step = pl.program_id(0)
-    head = dwk_ref.shape[1]
-
-    def part(rows):
-        return pl.ds(pl.multiple_of(step * rows, rows), rows)
-    for src, dst in ((out_in, out_ref), (dx_in, dx_ref), (dwo_in, dwo_ref), (dwq_in, dwq_ref)):
-        dst[...] = src[part(dst.shape[0]), :]
-    dw_ref[...] = dw_in[...]
-    a = a_ref[part(dwk_ref.shape[0]), :]
-    dwk_ref[...] = dot_nn(a, dkv_ref[:, :head])
-    dwv_ref[...] = dot_nn(a, dkv_ref[:, head:])
+                  out_ref, dx_ref, dwo_ref, dwq_ref, dw_ref, dwk_ref, dwv_ref, dwk, dwv, sems):
+    head = dwk.shape[1]
+    copies = []
+
+    def put(src, dst):
+        copies.append(pltpu.make_async_copy(src, dst, sems.at[len(copies)]))
+        copies[-1].start()
+
+    tiles = [pl.ds(row, STRIP) for row in range(0, dwk.shape[0], STRIP)]
+    for src, dst in ((out_in, out_ref), (dx_in, dx_ref), (dwo_in, dwo_ref), (dwq_in, dwq_ref), (dw_in, dw_ref)):
+        put(src, dst)
+    for rows in tiles:
+        a = a_ref[rows, :]
+        for grad, cols, dst in ((dwk, slice(0, head), dwk_ref), (dwv, slice(head, 2 * head), dwv_ref)):
+            grad[rows, :] = dot_nn(a, dkv_ref[:, cols])
+            put(grad.at[rows], dst.at[rows])
+    for copy in copies:
+        copy.wait()
 
 
 def local_block(size, stride, hidden, positions, norm_w, w_query, w_key, w_value, w_out, grad_out):
@@ -652,9 +662,10 @@
         functools.partial(block_kernel, size, stride),
         out_shape=[V((block, width), BF16), V((block, width), BF16), V((head, width), F32), V((width, head), F32), V(small, F32),
                    V((seq, width), BF16), V((seq, kv), BF16), shape(full, BF16), shape(full, BF16)],
-        in_specs=[vm] * 3 + [hbm] * 6,
+        in_specs=[hbm] * 9,
         out_specs=[vm] * 7 + [hbm] * 2,
-        scratch_shapes=[V((block, width), BF16), V((parts, part_rows, width), BF16), V((1, width), F32),
+        scratch_shapes=[V(small, F32), V((1, seq), jnp.int32), V((1, half), F32),
+                        V((block, width), BF16), V((parts, part_rows, width), BF16), V((1, width), F32),
                         V(full, BF16), V((3, width, head), BF16), V((parts, part_rows, width), BF16),
                         V((parts, part_rows, width), BF16)] + [V((seq, head), BF16)] * 5
         + [V((seq, kv), F32), V((size, block, head), BF16), V((size, block, head), BF16),
@@ -662,25 +673,20 @@
            V((TILE, 128), F32), V((TILE, 128), F32), V((TILE, head), F32),
            V((4, block, kv), F32), V((3, block, kv), F32), V((block // 2, kv), F32), V((block // 2, kv), F32),
            V((block, kv), F32), V((block, kv), F32), V((head, width), F32), V((1, width), F32),
-           V((size, width // 128, 128), F32), dma((8,))]
+           V((size, width // 128, 128), F32), dma((8,)), dma((3,))]
         + [dma((13,))] * 10 + [dma((8,))] * 4 + [dma((9,))] * 4 + [dma((10,))] * 2 + [dma((size,))] * 2,
         compiler_params=pltpu.CompilerParams(collective_id=0, has_side_effects=True, vmem_limit_bytes=VMEM_LIMIT - KEPT),
         name='attention_block',
     )(norm_w.reshape(width // lanes, lanes), positions, inv_freq, x, dout, w_query, w_key, w_value,
       w_out.reshape(parts, part_rows, width))
 
-    steps = width // COLS
-    whole = lambda *dims: pl.BlockSpec(dims, lambda n: (0, 0))
-    rows = lambda *dims: pl.BlockSpec(dims, lambda n: (n, 0))
-    passed = [rows(block // steps, width), rows(block // steps, width), rows(head // steps, width), rows(width // steps, head),
-              whole(*small)]
-    dwk, dwv, out, dx, dwo, dwq, dw = pl.pallas_call(
+    out, dx, dwo, dwq, dw, dwk, dwv = pl.pallas_call(
         weight_kernel,
-        grid=(steps,),
-        out_shape=[shape((width, head), F32)] * 2 + [shape((block, width), BF16)] * 2
-        + [shape((head, width), F32), shape((width, head), F32), shape(small, F32)],
+        out_shape=[shape((block, width), BF16)] * 2 + [shape((head, width), F32), shape((width, head), F32), shape(small, F32)]
+        + [shape((width, head), F32)] * 2,
         in_specs=[vm] * 7,
-        out_specs=[rows(width // steps, head)] * 2 + passed,
+        out_specs=[hbm] * 7,
+        scratch_shapes=[V((width, head), F32), V((width, head), F32), dma((5 + 2 * (width // STRIP),))],
         compiler_params=pltpu.CompilerParams(vmem_limit_bytes=VMEM_LIMIT - KEPT),
         name='weight_grads',
     )(*[pltpu.with_memory_space_constraint(v, V) for v in results])

time: 153 us -> 152 us (level)
  no operation moved by 1% of the time
where the time goes in v6:
time: 152 us; the launch traced here: 151 us
  Pallas kernels  151 us (99%)
    pallas_call x1, Pallas kernels, local_block(): pl.pallas_call(functools.partial(block_kernel, size, stride), out_shape=[...  145 us
    pallas_call x1, Pallas kernels, local_block(): pl.pallas_call(weight_kernel, out_shape=[shape((block, width), BF16)] * 2...  5.46 us

profile of v6, /device:TPU:81, one launch (start us, length us, event | category | flops | bytes accessed | tf_op | source)
XLA Modules:
  0.0 151.4 jit_solution(8329933840155527608)
XLA Ops:
  0.6 145.1 %attention_block.1 = (bf16[256,2048]{1,0:T(8,128)(2,1)S(1)}, bf16[256,2048]{1,0:T(8,128)(2,1)S(1)}, f32[256,2048]{1,0:T(8,128)S(1)}, f32[2048,256]{1,0:T(8,128)S...) custom-call(f32[16,128]{1,0:T(8,128)} %bitcast.10, ...), custom_call_target="tpu_custom_call" | custom-call | tf_op jit(solution)/shard_map/attention_block/pallas_call | solution.py:661
  145.8 5.5 %weight_grads.1 = (bf16[256,2048]{1,0:T(8,128)(2,1)}, bf16[256,2048]{1,0:T(8,128)(2,1)}, f32[256,2048]{1,0:T(8,128)}, f32[2048,256]{1,0:T(8,128)}, f32[16,128]{1...) custom-call(bf16[256,2048]{1,0:T(8,128)(2,1)S(1)} %get-tuple-element.21.out_in, ...), custom_call_target="tpu_custom_call" | custom-call | tf_op jit(solution)/shard_map/weight_grads/pallas_call | solution.py:683

commit v7 on v6

--- a/solution.py
+++ b/solution.py
@@ -15,7 +15,7 @@
 STRIP = 256
 COLS = 512
 VMEM_LIMIT = 63 * 1024 * 1024
-KEPT = 16 * 1024 * 1024
+KEPT = 18 * 1024 * 1024
 
 
 def dot_nn(a, b):
@@ -284,7 +284,7 @@
 
 
 def block_kernel(size, stride, norm_hbm, pos_hbm, freq_hbm, x_hbm, dout_hbm, wq_hbm, wk_hbm, wv_hbm, wo_hbm,
-                 out_ref, dx_ref, dwo_ref, dwq_ref, dw_ref, act_full, dkv_full, wo_full, wq_full,
+                 out_ref, dx_ref, dwo_ref, dwq_ref, dw_ref, act_full, dkv_full, dwv_ref, wo_full, wq_full,
                  norm_ref, pos_ref, freq_ref, x_ref, dout_ref, gain_ref, big, wbuf, wo, wqt, q_ref, k_ref, v_ref, o_ref, dq_ref, dkv_ref, o_all, dq_all,
                  relay_o, relay_q, lse_ref, cos_ref, sin_ref, m_scr, l_scr, acc,
                  d2d, sums, top, bot, from_l, from_r, wide, dw_me, dw_all, lsem, ssem,
@@ -308,15 +308,10 @@
         ((x_hbm, x_ref), (wq_hbm, wbuf.at[0]), (wo_hbm, wo), (dout_hbm, dout_ref), (wk_hbm, wbuf.at[1]), (wv_hbm, wbuf.at[2])))]
     small = [pltpu.make_async_copy(src, dst, ssem.at[i]) for i, (src, dst) in enumerate(
         ((norm_hbm, norm_ref), (pos_hbm, pos_ref), (freq_hbm, freq_ref)))]
-    for copy in (*small, load_x, load_wq, load_wo, load_dout, *load_kv):
+    for copy in (load_wq, load_wo, load_x, *small, load_dout, *load_kv):
         copy.start()
-    for copy in small:
-        copy.wait()
     lanes = 128
     groups = [slice(t * lanes, (t + 1) * lanes) for t in range(width // lanes)]
-    for t, cols in enumerate(groups):
-        gain_ref[:, cols] = 1.0 + norm_ref[t:t + 1, :]
-
     def weight_at(full):
         quarter = part_rows // 2
 
@@ -346,16 +341,16 @@
     dq_x = Exchange(p, block, dq_ref, dq_all, relay_q, ss_q, rs_q)
     kv_r = Scatter(p, block, dkv_ref, d2d, sums, top, bot, from_l, from_r, ss_r, rs_r)
 
-    def start_weight(g, shard, src, sem):
+    def start_weight(g, shard, src, sem, load):
         quarter = part_rows // 2
         g.start([src.at[p.part, pl.ds(h * quarter, quarter)] for h in (0, 1)], src.at[p.part])
+        load.wait()
         own = pltpu.make_async_copy(shard.at[p.part], g.own_all, lsem.at[sem])
         own.start()
         return own
 
     pl.semaphore_wait(barrier, size + 1)
-    load_wo.wait()
-    own_wo = start_weight(wo_g, wo, wo_hbm, 6)
+    own_wo = start_weight(wo_g, wo, wo_hbm, 6, load_wo)
     load_wq.wait()
 
     @pl.loop(0, width // COLS)
@@ -364,9 +359,11 @@
         flipped = wbuf[0, rows, :].T
         for g in range(parts):
             wqt[g, :, rows] = flipped[g * part_rows:(g + 1) * part_rows, :]
-    own_wq = start_weight(wq_g, wqt, wqt, 7)
-
-    load_x.wait()
+    own_wq = start_weight(wq_g, wqt, wqt, 7, load_x)
+    for copy in small:
+        copy.wait()
+    for t, cols in enumerate(groups):
+        gain_ref[:, cols] = 1.0 + norm_ref[t:t + 1, :]
 
     @pl.loop(0, block // 64)
     def _(n):
@@ -603,13 +600,18 @@
     for d in range(1, size):
         remote(dw_all.at[p.me], dw_all.at[p.me], ss_w.at[d], rs_w.at[d], peers[d - 1]).start()
     kv_g.second()
+    kv_g.sibling_near()
+
+    def weight_v(cols):
+        dwv_ref[cols, :] = sum(dot_nn(act_full[cols, tokens], dkv_full[tokens, head:])
+                               for tokens in (rows_of(chip * TILE, TILE) for chip in (p.chip_l, p.chip_r)))
+    col_tiles(weight_v)
     kv_g.third()
     for d in range(1, size):
         source = dw_all.at[lax.rem(p.me + size - d, size)]
         remote(source, source, ss_w.at[d], rs_w.at[d], p.sib).wait_recv()
     dw_ref[...] = jnp.sum(dw_all[...], axis=0)
     kv_g.sibling()
-    kv_g.sibling_near()
     kv_g.sibling_far()
 
     for d in range(1, size):
@@ -618,9 +620,11 @@
         g.finish()
 
 
-def weight_kernel(out_in, dx_in, dwo_in, dwq_in, dw_in, a_ref, dkv_ref,
+def weight_kernel(chips, out_in, dx_in, dwo_in, dwq_in, dw_in, a_ref, dkv_ref, dwv_in,
                   out_ref, dx_ref, dwo_ref, dwq_ref, dw_ref, dwk_ref, dwv_ref, dwk, dwv, sems):
     head = dwk.shape[1]
+    chip = lax.div(lax.axis_index('tp'), 2)
+    left_out = [rows_of(c * TILE, TILE) for c in (chip, lax.rem(chip + 2, chips))]
     copies = []
 
     def put(src, dst):
@@ -631,10 +635,10 @@
     for src, dst in ((out_in, out_ref), (dx_in, dx_ref), (dwo_in, dwo_ref), (dwq_in, dwq_ref), (dw_in, dw_ref)):
         put(src, dst)
     for rows in tiles:
-        a = a_ref[rows, :]
-        for grad, cols, dst in ((dwk, slice(0, head), dwk_ref), (dwv, slice(head, 2 * head), dwv_ref)):
-            grad[rows, :] = dot_nn(a, dkv_ref[:, cols])
-            put(grad.at[rows], dst.at[rows])
+        dwk[rows, :] = dot_nn(a_ref[rows, :], dkv_ref[:, :head])
+        put(dwk.at[rows], dwk_ref.at[rows])
+        dwv[rows, :] = dwv_in[rows, :] + sum(dot_nn(a_ref[rows, tokens], dkv_ref[tokens, head:]) for tokens in left_out)
+        put(dwv.at[rows], dwv_ref.at[rows])
     for copy in copies:
         copy.wait()
 
@@ -661,9 +665,9 @@
     *results, _, _ = pl.pallas_call(
         functools.partial(block_kernel, size, stride),
         out_shape=[V((block, width), BF16), V((block, width), BF16), V((head, width), F32), V((width, head), F32), V(small, F32),
-                   V((seq, width), BF16), V((seq, kv), BF16), shape(full, BF16), shape(full, BF16)],
+                   V((seq, width), BF16), V((seq, kv), BF16), V((width, head), F32), shape(full, BF16), shape(full, BF16)],
         in_specs=[hbm] * 9,
-        out_specs=[vm] * 7 + [hbm] * 2,
+        out_specs=[vm] * 8 + [hbm] * 2,
         scratch_shapes=[V(small, F32), V((1, seq), jnp.int32), V((1, half), F32),
                         V((block, width), BF16), V((parts, part_rows, width), BF16), V((1, width), F32),
                         V(full, BF16), V((3, width, head), BF16), V((parts, part_rows, width), BF16),
@@ -681,10 +685,10 @@
       w_out.reshape(parts, part_rows, width))
 
     out, dx, dwo, dwq, dw, dwk, dwv = pl.pallas_call(
-        weight_kernel,
+        functools.partial(weight_kernel, chips),
         out_shape=[shape((block, width), BF16)] * 2 + [shape((head, width), F32), shape((width, head), F32), shape(small, F32)]
         + [shape((width, head), F32)] * 2,
-        in_specs=[vm] * 7,
+        in_specs=[vm] * 8,
         out_specs=[hbm] * 7,
         scratch_shapes=[V((width, head), F32), V((width, head), F32), dma((5 + 2 * (width // STRIP),))],
         compiler_params=pltpu.CompilerParams(vmem_limit_bytes=VMEM_LIMIT - KEPT),

time: 152 us -> 151 us (level)
  no operation moved by 1% of the time
where the time goes in v7:
time: 151 us; the launch traced here: 150 us
  Pallas kernels  150 us (99%)
    pallas_call x1, Pallas kernels, local_block(): pl.pallas_call(functools.partial(block_kernel, size, stride), out_shape=[...  145 us
    pallas_call x1, Pallas kernels, local_block(): pl.pallas_call(functools.partial(weight_kernel, chips), out_shape=[shape(...  4.45 us

profile of v7, /device:TPU:81, one launch (start us, length us, event | category | flops | bytes accessed | tf_op | source)
XLA Modules:
  0.0 150.4 jit_solution(10340446890033150073)
XLA Ops:
  0.6 145.1 %attention_block.1 = (bf16[256,2048]{1,0:T(8,128)(2,1)S(1)}, bf16[256,2048]{1,0:T(8,128)(2,1)S(1)}, f32[256,2048]{1,0:T(8,128)S(1)}, f32[2048,256]{1,0:T(8,128)S...) custom-call(f32[16,128]{1,0:T(8,128)} %bitcast.10, ...), custom_call_target="tpu_custom_call" | custom-call | tf_op jit(solution)/shard_map/attention_block/pallas_call | solution.py:665
  145.8 4.4 %weight_grads.1 = (bf16[256,2048]{1,0:T(8,128)(2,1)}, bf16[256,2048]{1,0:T(8,128)(2,1)}, f32[256,2048]{1,0:T(8,128)}, f32[2048,256]{1,0:T(8,128)}, f32[16,128]{1...) custom-call(bf16[256,2048]{1,0:T(8,128)(2,1)S(1)} %get-tuple-element.22.out_in, ...), custom_call_target="tpu_custom_call" | custom-call | tf_op jit(solution)/shard_map/weight_grads/pallas_call | solution.py:687

commit v8 on v7

--- a/solution.py
+++ b/solution.py
@@ -15,7 +15,7 @@
 STRIP = 256
 COLS = 512
 VMEM_LIMIT = 63 * 1024 * 1024
-KEPT = 18 * 1024 * 1024
+KEPT = 20 * 1024 * 1024
 
 
 def dot_nn(a, b):
@@ -100,8 +100,9 @@
             self._send(7 + k, self.regions[k], self.regions[k], 7 + k, self.p.sib)
 
     def _forward(self, *which):
-        self.recv(*which)
-        self._forward_only(*which)
+        for k in which:
+            self.recv(k)
+            self._forward_only(k)
 
     def first(self):
         self.recv(0, 3)
@@ -284,7 +285,7 @@
 
 
 def block_kernel(size, stride, norm_hbm, pos_hbm, freq_hbm, x_hbm, dout_hbm, wq_hbm, wk_hbm, wv_hbm, wo_hbm,
-                 out_ref, dx_ref, dwo_ref, dwq_ref, dw_ref, act_full, dkv_full, dwv_ref, wo_full, wq_full,
+                 out_ref, dx_ref, dwo_ref, dwq_ref, dw_ref, act_full, dkv_full, dwkv_ref, wo_full, wq_full,
                  norm_ref, pos_ref, freq_ref, x_ref, dout_ref, gain_ref, big, wbuf, wo, wqt, q_ref, k_ref, v_ref, o_ref, dq_ref, dkv_ref, o_all, dq_all,
                  relay_o, relay_q, lse_ref, cos_ref, sin_ref, m_scr, l_scr, acc,
                  d2d, sums, top, bot, from_l, from_r, wide, dw_me, dw_all, lsem, ssem,
@@ -602,10 +603,10 @@
     kv_g.second()
     kv_g.sibling_near()
 
-    def weight_v(cols):
-        dwv_ref[cols, :] = sum(dot_nn(act_full[cols, tokens], dkv_full[tokens, head:])
-                               for tokens in (rows_of(chip * TILE, TILE) for chip in (p.chip_l, p.chip_r)))
-    col_tiles(weight_v)
+    def weight_kv(cols):
+        dwkv_ref[cols, :] = sum(dot_nn(act_full[cols, tokens], dkv_full[tokens, :])
+                                for tokens in (rows_of(chip * TILE, TILE) for chip in (p.chip_l, p.chip_r)))
+    col_tiles(weight_kv)
     kv_g.third()
     for d in range(1, size):
         source = dw_all.at[lax.rem(p.me + size - d, size)]
@@ -620,7 +621,7 @@
         g.finish()
 
 
-def weight_kernel(chips, out_in, dx_in, dwo_in, dwq_in, dw_in, a_ref, dkv_ref, dwv_in,
+def weight_kernel(chips, out_in, dx_in, dwo_in, dwq_in, dw_in, a_ref, dkv_ref, dwkv_in,
                   out_ref, dx_ref, dwo_ref, dwq_ref, dw_ref, dwk_ref, dwv_ref, dwk, dwv, sems):
     head = dwk.shape[1]
     chip = lax.div(lax.axis_index('tp'), 2)
@@ -635,9 +636,9 @@
     for src, dst in ((out_in, out_ref), (dx_in, dx_ref), (dwo_in, dwo_ref), (dwq_in, dwq_ref), (dw_in, dw_ref)):
         put(src, dst)
     for rows in tiles:
-        dwk[rows, :] = dot_nn(a_ref[rows, :], dkv_ref[:, :head])
+        dwk[rows, :] = dwkv_in[rows, :head] + sum(dot_nn(a_ref[rows, tokens], dkv_ref[tokens, :head]) for tokens in left_out)
         put(dwk.at[rows], dwk_ref.at[rows])
-        dwv[rows, :] = dwv_in[rows, :] + sum(dot_nn(a_ref[rows, tokens], dkv_ref[tokens, head:]) for tokens in left_out)
+        dwv[rows, :] = dwkv_in[rows, head:] + sum(dot_nn(a_ref[rows, tokens], dkv_ref[tokens, head:]) for tokens in left_out)
         put(dwv.at[rows], dwv_ref.at[rows])
     for copy in copies:
         copy.wait()
@@ -665,7 +666,7 @@
     *results, _, _ = pl.pallas_call(
         functools.partial(block_kernel, size, stride),
         out_shape=[V((block, width), BF16), V((block, width), BF16), V((head, width), F32), V((width, head), F32), V(small, F32),
-                   V((seq, width), BF16), V((seq, kv), BF16), V((width, head), F32), shape(full, BF16), shape(full, BF16)],
+                   V((seq, width), BF16), V((seq, kv), BF16), V((width, kv), F32), shape(full, BF16), shape(full, BF16)],
         in_specs=[hbm] * 9,
         out_specs=[vm] * 8 + [hbm] * 2,
         scratch_shapes=[V(small, F32), V((1, seq), jnp.int32), V((1, half), F32),

time: 151 us -> 150 us (level)
  no operation moved by 1% of the time
where the time goes in v8:
time: 150 us
  Pallas kernels  149 us (99%)
    pallas_call x1, Pallas kernels, local_block(): pl.pallas_call(functools.partial(block_kernel, size, stride), out_shape=[...  145 us
    pallas_call x1, Pallas kernels, local_block(): pl.pallas_call(functools.partial(weight_kernel, chips), out_shape=[shape(...  4.11 us

profile of v8, /device:TPU:81, one launch (start us, length us, event | category | flops | bytes accessed | tf_op | source)
XLA Modules:
  0.0 150.1 jit_solution(14025027492611936161)
XLA Ops:
  0.6 145.1 %attention_block.1 = (bf16[256,2048]{1,0:T(8,128)(2,1)S(1)}, bf16[256,2048]{1,0:T(8,128)(2,1)S(1)}, f32[256,2048]{1,0:T(8,128)S(1)}, f32[2048,256]{1,0:T(8,128)S...) custom-call(f32[16,128]{1,0:T(8,128)} %bitcast.10, ...), custom_call_target="tpu_custom_call" | custom-call | tf_op jit(solution)/shard_map/attention_block/pallas_call | solution.py:666
  145.8 4.1 %weight_grads.1 = (bf16[256,2048]{1,0:T(8,128)(2,1)}, bf16[256,2048]{1,0:T(8,128)(2,1)}, f32[256,2048]{1,0:T(8,128)}, f32[2048,256]{1,0:T(8,128)}, f32[16,128]{1...) custom-call(bf16[256,2048]{1,0:T(8,128)(2,1)S(1)} %get-tuple-element.22.out_in, ...), custom_call_target="tpu_custom_call" | custom-call | tf_op jit(solution)/shard_map/weight_grads/pallas_call | solution.py:688
